TPU v7x, 256 devices: a whole 4x4x8 slice. The times are simulated.
256 devices in a mesh: rows: 128 (over y_lo, x, z, core), feat: 2 (over y_hi).
Axes of the slice: x: 4, y: 4 (y_hi: 2, y_lo: 2; y = y_hi * 2 + y_lo), z: 8, core: 2. Of those that a mesh axis runs over, the one named last changes fastest.
Arguments:
- train_cells: bfloat16 [8192, 1536], P('rows', 'feat'), may hold values from -24 to 24
- test_cells: bfloat16 [4096, 1536], P('rows', 'feat'), may hold values from -24 to 24
- feat_weights: bfloat16 [4, 192, 192], replicated
- row_weights: bfloat16 [4, 192, 192], replicated
- mlp_up: bfloat16 [192, 768], replicated, may hold values from -0.4375 to 0.4375
- mlp_down: bfloat16 [768, 192], replicated, may hold values from -0.21875 to 0.21875
Outputs:
- train_out: bfloat16 [8192, 1536], P('rows', 'feat')
- test_out: bfloat16 [4096, 1536], P('rows', 'feat')
All inputs are finite; a program needn't handle non-finite values.
Results may differ from a plain program's by a relative error of at most 0.017.
Values may be sent and summed in bfloat16 or wider, within the bound.
A program may use at most 128 MiB of HBM per device.

v0:
```python
import jax
import jax.numpy as jnp
from jax import lax
from jax.sharding import PartitionSpec as P

E = 192
HEADS = 6
HD = 32


eps_norm = 1e-05
far_below = -1e30


def layer_norm(values_in):
    centred = values_in - jnp.mean(values_in, axis=-1, keepdims=True)
    spread = jnp.mean(centred * centred, axis=-1, keepdims=True)
    return centred * lax.rsqrt(spread + eps_norm)


def project(normed, weight):
    height = normed.shape[0]
    return jnp.dot(normed.reshape(-1, E), weight, preferred_element_type=jnp.float32).reshape(
        height, -1
    )


def project_major(table, weight):
    return jnp.dot(table, weight, preferred_element_type=jnp.float32).astype(jnp.bfloat16)


def split_heads(table):
    return table.reshape(table.shape[0], -1, HEADS, HD)


def feature_major(table):
    return jnp.transpose(table.reshape(table.shape[0], -1, E), (1, 0, 2))


def feature_attention(queries, key_table, value_table):
    height = queries.shape[0]
    scores = jnp.einsum(
        "rqhd,rkhd->rhqk",
        split_heads(queries),
        split_heads(key_table),
        preferred_element_type=jnp.float32,
    ) * HD ** (-0.5)
    row_peak = jnp.max(scores, axis=-1, keepdims=True)
    weights = jnp.exp(scores - row_peak)
    totals = jnp.sum(weights, axis=-1)
    mixture = jnp.einsum(
        "rhqk,rkhd->rqhd",
        weights.astype(jnp.bfloat16),
        split_heads(value_table),
        preferred_element_type=jnp.float32,
    )
    mixture = mixture / jnp.transpose(totals, (0, 2, 1))[..., None]
    return mixture.astype(jnp.bfloat16).reshape(height, -1)


def attend_block(state, queries, key_block, value_block):
    weighted, running, totals = state
    scores = jnp.einsum(
        "fkhd,qfhd->fhkq", key_block, queries, preferred_element_type=jnp.float32
    ) * HD ** (-0.5)
    raised = jnp.maximum(running, jnp.max(scores, axis=-2))
    fading = jnp.exp(running - raised)
    weights = jnp.exp(scores - raised[..., None, :])
    totals = totals * fading + jnp.sum(weights, axis=-2)
    update = jnp.einsum(
        "fhkq,fkhd->qfhd",
        weights.astype(jnp.bfloat16),
        value_block,
        preferred_element_type=jnp.float32,
    )
    weighted = weighted * jnp.transpose(fading, (2, 0, 1))[..., None] + update
    return (weighted, raised, totals)


def absorb(state, queries, key_table, value_table):
    groups = key_table.shape[0]
    length = key_table.shape[1]
    span = 512
    number = length // span

    def advance(index, carried):
        key_block = lax.dynamic_slice_in_dim(key_table, index * span, span, 1).reshape(
            groups, span, HEADS, HD
        )
        value_block = lax.dynamic_slice_in_dim(value_table, index * span, span, 1).reshape(
            groups, span, HEADS, HD
        )
        return attend_block(carried, queries, key_block, value_block)

    return lax.fori_loop(0, number, advance, state)


def start_state(height, groups):
    return (
        jnp.zeros((height, groups, HEADS, HD), jnp.float32),
        jnp.full((groups, HEADS, height), far_below, jnp.float32),
        jnp.zeros((groups, HEADS, height), jnp.float32),
    )


def finish(state):
    weighted, running, totals = state
    return (weighted / jnp.transpose(totals, (2, 0, 1))[..., None]).astype(jnp.bfloat16)


def spread_copies(table, copies):
    major = feature_major(table)
    return jnp.broadcast_to(major[None], (copies,) + major.shape).reshape(-1, E)


def body(train_cells, test_cells, feat_weights, row_weights, mlp_up, mlp_down):
    train_height = train_cells.shape[0]
    joined = jnp.concatenate([train_cells, test_cells], axis=0)
    height = joined.shape[0]
    width = joined.shape[1]
    groups = width // E
    start_cells = joined.astype(jnp.float32).reshape(height, groups, E)
    normed_one = layer_norm(start_cells).astype(jnp.bfloat16).reshape(height, width)
    whole_rows = lax.all_to_all(normed_one, "feat", split_axis=0, concat_axis=1, tiled=True)
    row_queries = project(whole_rows, feat_weights[0]).astype(jnp.bfloat16)
    row_keys = project(whole_rows, feat_weights[1]).astype(jnp.bfloat16)
    row_values = project(whole_rows, feat_weights[2]).astype(jnp.bfloat16)
    mixture = feature_attention(row_queries, row_keys, row_values)
    moved = project(mixture, feat_weights[3]).astype(jnp.bfloat16)
    feat_out = lax.all_to_all(moved, "feat", split_axis=1, concat_axis=0, tiled=True)
    after_feat = start_cells + feat_out.astype(jnp.float32).reshape(height, groups, E)
    normed_two = layer_norm(after_feat).astype(jnp.bfloat16).reshape(height, width)
    row_query = project(normed_two, row_weights[0]).astype(jnp.bfloat16)
    train_normed = normed_two[:train_height]
    members = lax.axis_size("rows")
    copies = members // groups
    share = height // copies
    received = lax.all_to_all(
        spread_copies(train_normed, copies), "rows", split_axis=0, concat_axis=0, tiled=True
    )
    key_table = project_major(received, row_weights[1])
    value_table = project_major(received, row_weights[2])
    key_single = key_table[None]
    value_single = value_table[None]
    query_pieces = jnp.transpose(row_query.reshape(copies, share, groups, E), (0, 2, 1, 3)).reshape(
        members, share, E
    )
    received_queries = lax.all_to_all(query_pieces, "rows", split_axis=0, concat_axis=0, tiled=True)
    count = received_queries.shape[1]
    flat = received_queries.reshape(-1, 1, HEADS, HD)
    state = absorb(start_state(flat.shape[0], 1), flat, key_single, value_single)
    mixed = finish(state).reshape(members, count, E)
    returned = lax.all_to_all(mixed, "rows", split_axis=0, concat_axis=0, tiled=True)
    row_mix = jnp.transpose(returned.reshape(copies, groups, share, E), (0, 2, 1, 3)).reshape(
        height, width
    )
    after_row = after_feat + project(row_mix, row_weights[3]).reshape(height, groups, E)
    normed_three = layer_norm(after_row).astype(jnp.bfloat16)
    hidden = jax.nn.gelu(
        jnp.dot(normed_three.reshape(-1, E), mlp_up, preferred_element_type=jnp.float32),
        approximate=False,
    ).astype(jnp.bfloat16)
    lowered = jnp.dot(hidden, mlp_down, preferred_element_type=jnp.float32).reshape(
        height, groups, E
    )
    result = (after_row + lowered).astype(jnp.bfloat16).reshape(height, width)
    return (result[:train_height], result[train_height:])


def solution(mesh):
    return jax.shard_map(
        body,
        mesh=mesh,
        in_specs=(P("rows", "feat"), P("rows", "feat"), P(), P(), P(), P()),
        out_specs=(P("rows", "feat"), P("rows", "feat")),
        check_vma=False,
    )
```

profile of v0, /device:TPU:1, one launch (start us, length us, event | category | flops | bytes accessed | tf_op | source)
XLA Modules:
  0.0 342.0 jit_solution(15792970976832911742)
XLA Ops:
  0.7 1.1 concatenate.11
  5.0 5.0 %all-to-all-start = ((bf16[2,48,768]{2,1,0:T(8,128)(2,1)}), bf16[2,48,768]{2,1,0:T(8,128)(2,1)S(1)}, u32[]{:S(2)}, u32[]{:S(2)}) async-start(bf16[2,48,768]{2,1,0:T(8,128)(2,1)} %fusion.68), calls=%async_computation | async-start | bytes 294912 | tf_op jit(solution)/shard_map/all_to_all | solution.py:124
  10.3 4.6 %all-to-all-done = bf16[2,48,768]{2,1,0:T(8,128)(2,1)S(1)} async-done(((bf16[2,48,768]{2,1,0:T(8,128)(2,1)}), bf16[2,48,768]{2,1,0:T(8,128)(2,1)S(1)}, u32[]{:S(2)}, u32[]{:S(2)}) %all-to-all-start) | async-done | bytes 147488 | tf_op jit(solution)/shard_map/all_to_all | solution.py:124
  19.0 7.3 %all_to_all.45 = bf16[48,2,768]{2,0,1:T(8,128)(2,1)S(1)} all-to-all(bf16[48,2,768]{2,0,1:T(8,128)(2,1)S(1)} %copy.49), channel_id=1, replica_groups=mesh['rows'=128,'feat'=2] {'feat'}, dimensions={1} | all-to-all | bytes 294912 | tf_op jit(solution)/shard_map/all_to_all | solution.py:130
  28.6 15.6 %all-to-all-start.3 = ((bf16[128,3,192]{2,1,0:T(4,128)(2,1)}), bf16[128,3,192]{2,1,0:T(4,128)(2,1)S(1)}, u32[]{:S(2)}, u32[]{:S(2)}) async-start(bf16[128,3,192]{2,1,0:T(4,128)(2,1)} %bitcast.29), calls=%async_computation.3 | async-start | bytes 524288 | tf_op jit(solution)/shard_map/all_to_all | solution.py:148
  44.3 13.5 %all-to-all-done.3 = bf16[128,3,192]{2,1,0:T(4,128)(2,1)S(1)} async-done(((bf16[128,3,192]{2,1,0:T(4,128)(2,1)}), bf16[128,3,192]{2,1,0:T(4,128)(2,1)S(1)}, u32[]{:S(2)}, u32[]{:S(2)}) %all-to-all-start.3) | async-done | bytes 147488 | tf_op jit(solution)/shard_map/all_to_all | solution.py:148
  57.7 2.5 broadcast_in_dim.21
  60.2 6.7 %all-to-all-start.2 = ((bf16[128,64,192]{2,1,0:T(8,128)(2,1)}), bf16[128,64,192]{2,1,0:T(8,128)(2,1)}, u32[]{:S(2)}, u32[]{:S(2)}) async-start(bf16[128,64,192]{2,1,0:T(8,128)(2,1)} %bitcast.143), calls=%async_computation.2 | async-start | bytes 8388608 | tf_op jit(solution)/shard_map/all_to_all | solution.py:138
  67.8 94.1 %all-to-all-done.2 = bf16[128,64,192]{2,1,0:T(8,128)(2,1)} async-done(((bf16[128,64,192]{2,1,0:T(8,128)(2,1)}), bf16[128,64,192]{2,1,0:T(8,128)(2,1)}, u32[]{:S(2)}, u32[]{:S(2)}) %all-to-all-start.2) | async-done | bytes 3145760 | tf_op jit(solution)/shard_map/all_to_all | solution.py:138
  162.0 5.4 %fusion.14 = bf16[1,8192,192]{1,2,0:T(8,128)(2,1)} fusion(bf16[8192,192]{1,0:T(8,128)(2,1)} %bitcast.21, bf16[4,192,192]{2,1,0:T(8,128)(2,1)S(1)} %copy-done.2), kind=kOutput, calls=%fused_computation.20 | convolution fusion | flops 605552640 | bytes 6389760 | tf_op jit(solution)/shard_map/dot_general | solution.py:29
  167.3 5.5 %fusion.15 = bf16[1,8192,192]{1,2,0:T(8,128)(2,1)} fusion(bf16[8192,192]{1,0:T(8,128)(2,1)} %bitcast.21, bf16[4,192,192]{2,1,0:T(8,128)(2,1)S(1)} %copy-done.2), kind=kOutput, calls=%fused_computation.21 | convolution fusion | flops 605552640 | bytes 6389760 | tf_op jit(solution)/shard_map/dot_general | solution.py:29
  172.8 139.9 %while.18 = (s32[]{:T(128)}, f32[384,1,6,32]{0,3,2,1:T(8,128)S(1)}, f32[1,6,384]{2,1,0:T(8,128)S(1)}, f32[1,6,384]{2,1,0:T(8,128)S(1)}, bf16[1,8192,192]{1,2,0:T...) while((s32[]{:T(128)}, f32[384,1,6,32]{0,3,2,1:T(8,128)S(1)}, ...), condition=%wide.region_9.0_spmd.clone, body=%wide.region_6.0_spmd.clone.sunk | while | flops 160667136 | bytes 35094724 | solution.py:95
  172.8 1.0 constant_dynamic-slice_fusion.3
  173.8 2.9 multiply_reduce_fusion.4
  176.8 3.3 fusion.145
  181.5 1.1 constant_dynamic-slice_fusion.3
  182.6 2.9 multiply_reduce_fusion.4
  185.5 3.3 fusion.145
  190.3 1.1 constant_dynamic-slice_fusion.3
  191.3 2.9 multiply_reduce_fusion.4
  194.3 3.3 fusion.145
  199.0 1.1 constant_dynamic-slice_fusion.3
  200.1 2.9 multiply_reduce_fusion.4
  203.0 3.3 fusion.145
  207.8 1.1 constant_dynamic-slice_fusion.3
  208.8 2.9 multiply_reduce_fusion.4
  211.8 3.3 fusion.145
  216.5 1.1 constant_dynamic-slice_fusion.3
  217.6 2.9 multiply_reduce_fusion.4
  220.5 3.3 fusion.145
  225.2 1.1 constant_dynamic-slice_fusion.3
  226.3 2.9 multiply_reduce_fusion.4
  229.3 3.3 fusion.145
  234.0 1.1 constant_dynamic-slice_fusion.3
  235.0 2.9 multiply_reduce_fusion.4
  238.0 3.3 fusion.145
  241.8 0.9 fusion.144
  242.7 1.1 constant_dynamic-slice_fusion.3
  243.8 2.9 multiply_reduce_fusion.4
  246.8 3.3 fusion.145
  251.5 1.1 constant_dynamic-slice_fusion.3
  252.5 2.9 multiply_reduce_fusion.4
  255.5 3.3 fusion.145
  260.2 1.1 constant_dynamic-slice_fusion.3
  261.3 2.9 multiply_reduce_fusion.4
  264.2 3.3 fusion.145
  268.0 0.9 fusion.144
  269.0 1.1 constant_dynamic-slice_fusion.3
  270.0 2.9 multiply_reduce_fusion.4
  273.0 3.3 fusion.145
  277.7 1.1 constant_dynamic-slice_fusion.3
  278.8 2.9 multiply_reduce_fusion.4
  281.7 3.3 fusion.145
  286.4 1.1 constant_dynamic-slice_fusion.3
  287.5 2.9 multiply_reduce_fusion.4
  290.5 3.3 fusion.145
  295.2 1.1 constant_dynamic-slice_fusion.3
  296.2 2.9 multiply_reduce_fusion.4
  299.2 3.3 fusion.145
  303.9 1.1 constant_dynamic-slice_fusion.3
  305.0 2.9 multiply_reduce_fusion.4
  308.0 3.3 fusion.145
  313.8 21.9 %all_to_all.46 = bf16[128,3,192]{2,1,0:T(4,128)(2,1)S(1)} all-to-all(bf16[128,3,192]{2,1,0:T(4,128)(2,1)S(1)} %reshape.249), channel_id=1, replica_groups=mesh['rows'=128,'feat'=2] {'rows'}, dimensions={0} | all-to-all | bytes 294912 | tf_op jit(solution)/shard_map/all_to_all | solution.py:153
  337.1 3.0 fusion.28
  (172 shorter events, 35.6 us)
Async XLA Ops:
  0.6 336.3 %copy-start = (bf16[768,192]{0,1:T(8,128)(2,1)S(1)}, bf16[768,192]{0,1:T(8,128)(2,1)}, u32[]{:S(2)}) copy-start(bf16[768,192]{0,1:T(8,128)(2,1)} %param.13) | copy-start | bytes 884740
  0.6 2.6 copy-start.4
  0.7 2.6 copy-start.5
  3.8 6.1 %copy-start.3 = (bf16[4,192,192]{2,1,0:T(8,128)(2,1)S(1)}, bf16[4,192,192]{2,1,0:T(8,128)(2,1)}, u32[]{:S(2)}) copy-start(bf16[4,192,192]{2,1,0:T(8,128)(2,1)} %param.10) | copy-start | bytes 884740
  5.0 9.9 %all-to-all-start = ((bf16[2,48,768]{2,1,0:T(8,128)(2,1)}), bf16[2,48,768]{2,1,0:T(8,128)(2,1)S(1)}, u32[]{:S(2)}, u32[]{:S(2)}) async-start(bf16[2,48,768]{2,1,0:T(8,128)(2,1)} %fusion.68), calls=%async_computation | async-start | bytes 294912 | tf_op jit(solution)/shard_map/all_to_all | solution.py:124
  26.5 1.0 copy-start.2
  28.6 29.1 %all-to-all-start.3 = ((bf16[128,3,192]{2,1,0:T(4,128)(2,1)}), bf16[128,3,192]{2,1,0:T(4,128)(2,1)S(1)}, u32[]{:S(2)}, u32[]{:S(2)}) async-start(bf16[128,3,192]{2,1,0:T(4,128)(2,1)} %bitcast.29), calls=%async_computation.3 | async-start | bytes 524288 | tf_op jit(solution)/shard_map/all_to_all | solution.py:148
  60.2 101.7 %all-to-all-start.2 = ((bf16[128,64,192]{2,1,0:T(8,128)(2,1)}), bf16[128,64,192]{2,1,0:T(8,128)(2,1)}, u32[]{:S(2)}, u32[]{:S(2)}) async-start(bf16[128,64,192]{2,1,0:T(8,128)(2,1)} %bitcast.143), calls=%async_computation.2 | async-start | bytes 8388608 | tf_op jit(solution)/shard_map/all_to_all | solution.py:138
  176.8 3.8 %copy-start.1 = (f32[6,512,384]{2,1,0:T(8,128)S(1)}, f32[6,512,384]{2,1,0:T(8,128)}, u32[]{:S(2)}) copy-start(f32[6,512,384]{2,1,0:T(8,128)} %get-tuple-element.245) | copy-start | bytes 14155780 | tf_op jit(solution)/shard_map/while
  185.5 3.8 %copy-start.1 = (f32[6,512,384]{2,1,0:T(8,128)S(1)}, f32[6,512,384]{2,1,0:T(8,128)}, u32[]{:S(2)}) copy-start(f32[6,512,384]{2,1,0:T(8,128)} %get-tuple-element.245) | copy-start | bytes 14155780 | tf_op jit(solution)/shard_map/while
  194.3 3.8 %copy-start.1 = (f32[6,512,384]{2,1,0:T(8,128)S(1)}, f32[6,512,384]{2,1,0:T(8,128)}, u32[]{:S(2)}) copy-start(f32[6,512,384]{2,1,0:T(8,128)} %get-tuple-element.245) | copy-start | bytes 14155780 | tf_op jit(solution)/shard_map/while
  203.0 3.8 %copy-start.1 = (f32[6,512,384]{2,1,0:T(8,128)S(1)}, f32[6,512,384]{2,1,0:T(8,128)}, u32[]{:S(2)}) copy-start(f32[6,512,384]{2,1,0:T(8,128)} %get-tuple-element.245) | copy-start | bytes 14155780 | tf_op jit(solution)/shard_map/while
  211.8 3.8 %copy-start.1 = (f32[6,512,384]{2,1,0:T(8,128)S(1)}, f32[6,512,384]{2,1,0:T(8,128)}, u32[]{:S(2)}) copy-start(f32[6,512,384]{2,1,0:T(8,128)} %get-tuple-element.245) | copy-start | bytes 14155780 | tf_op jit(solution)/shard_map/while
  220.5 3.8 %copy-start.1 = (f32[6,512,384]{2,1,0:T(8,128)S(1)}, f32[6,512,384]{2,1,0:T(8,128)}, u32[]{:S(2)}) copy-start(f32[6,512,384]{2,1,0:T(8,128)} %get-tuple-element.245) | copy-start | bytes 14155780 | tf_op jit(solution)/shard_map/while
  229.3 3.8 %copy-start.1 = (f32[6,512,384]{2,1,0:T(8,128)S(1)}, f32[6,512,384]{2,1,0:T(8,128)}, u32[]{:S(2)}) copy-start(f32[6,512,384]{2,1,0:T(8,128)} %get-tuple-element.245) | copy-start | bytes 14155780 | tf_op jit(solution)/shard_map/while
  238.0 3.8 %copy-start.1 = (f32[6,512,384]{2,1,0:T(8,128)S(1)}, f32[6,512,384]{2,1,0:T(8,128)}, u32[]{:S(2)}) copy-start(f32[6,512,384]{2,1,0:T(8,128)} %get-tuple-element.245) | copy-start | bytes 14155780 | tf_op jit(solution)/shard_map/while
  246.7 3.8 %copy-start.1 = (f32[6,512,384]{2,1,0:T(8,128)S(1)}, f32[6,512,384]{2,1,0:T(8,128)}, u32[]{:S(2)}) copy-start(f32[6,512,384]{2,1,0:T(8,128)} %get-tuple-element.245) | copy-start | bytes 14155780 | tf_op jit(solution)/shard_map/while
  255.5 3.8 %copy-start.1 = (f32[6,512,384]{2,1,0:T(8,128)S(1)}, f32[6,512,384]{2,1,0:T(8,128)}, u32[]{:S(2)}) copy-start(f32[6,512,384]{2,1,0:T(8,128)} %get-tuple-element.245) | copy-start | bytes 14155780 | tf_op jit(solution)/shard_map/while
  264.2 3.8 %copy-start.1 = (f32[6,512,384]{2,1,0:T(8,128)S(1)}, f32[6,512,384]{2,1,0:T(8,128)}, u32[]{:S(2)}) copy-start(f32[6,512,384]{2,1,0:T(8,128)} %get-tuple-element.245) | copy-start | bytes 14155780 | tf_op jit(solution)/shard_map/while
  273.0 3.8 %copy-start.1 = (f32[6,512,384]{2,1,0:T(8,128)S(1)}, f32[6,512,384]{2,1,0:T(8,128)}, u32[]{:S(2)}) copy-start(f32[6,512,384]{2,1,0:T(8,128)} %get-tuple-element.245) | copy-start | bytes 14155780 | tf_op jit(solution)/shard_map/while
  281.7 3.8 %copy-start.1 = (f32[6,512,384]{2,1,0:T(8,128)S(1)}, f32[6,512,384]{2,1,0:T(8,128)}, u32[]{:S(2)}) copy-start(f32[6,512,384]{2,1,0:T(8,128)} %get-tuple-element.245) | copy-start | bytes 14155780 | tf_op jit(solution)/shard_map/while
  290.5 3.8 %copy-start.1 = (f32[6,512,384]{2,1,0:T(8,128)S(1)}, f32[6,512,384]{2,1,0:T(8,128)}, u32[]{:S(2)}) copy-start(f32[6,512,384]{2,1,0:T(8,128)} %get-tuple-element.245) | copy-start | bytes 14155780 | tf_op jit(solution)/shard_map/while
  299.2 3.8 %copy-start.1 = (f32[6,512,384]{2,1,0:T(8,128)S(1)}, f32[6,512,384]{2,1,0:T(8,128)}, u32[]{:S(2)}) copy-start(f32[6,512,384]{2,1,0:T(8,128)} %get-tuple-element.245) | copy-start | bytes 14155780 | tf_op jit(solution)/shard_map/while
  307.9 3.8 %copy-start.1 = (f32[6,512,384]{2,1,0:T(8,128)S(1)}, f32[6,512,384]{2,1,0:T(8,128)}, u32[]{:S(2)}) copy-start(f32[6,512,384]{2,1,0:T(8,128)} %get-tuple-element.245) | copy-start | bytes 14155780 | tf_op jit(solution)/shard_map/while
  336.1 1.0 copy-start.6
where the time goes:
time: 343 us; the launch traced here: 342 us
  waiting for transfers between devices  112 us (33%)
  matrix products  78.5 us (23%)
  other arithmetic  55.5 us (16%)
  local copies, waits for them, and re-layouts  37.2 us (11%)
  blocking collectives  29.2 us (9%)
  starting transfers between devices  27.3 us (8%)
    all_to_all x1, waiting for transfers between devices, body(): lax.all_to_all(spread_copies(train_normed, copies), 'rows', split_axis=0,...  94.1 us
    reduce_sum x16, other arithmetic, attend_block(): totals = totals * fading + jnp.sum(weights, axis=-2)  52.4 us
    dot_general x16, matrix products, attend_block(): jnp.einsum('fkhd,qfhd->fhkq', key_block, queries, preferred_element_type=...  47.2 us
    all_to_all x1, blocking collectives, body(): lax.all_to_all(mixed, 'rows', split_axis=0, concat_axis=0, tiled=True)  21.9 us
    dynamic_slice x16, local copies, waits for them, and re-layouts, advance(): lax.dynamic_slice_in_dim(value_table, index * span, span, 1)  16.9 us
    all_to_all x1, starting transfers between devices, body(): lax.all_to_all(query_pieces, 'rows', split_axis=0, concat_axis=0, tiled=T...  15.6 us
    dot_general x16, matrix products, attend_block(): jnp.einsum('fhkq,fkhd->qfhd', weights.astype(jnp.bfloat16), value_block,...  14.9 us
    all_to_all x1, waiting for transfers between devices, body(): lax.all_to_all(query_pieces, 'rows', split_axis=0, concat_axis=0, tiled=T...  13.5 us
  transfers between devices with their start and end apart: 3, of which 3 were waited for; matrix products, arithmetic and copies ran while one was open for 0% of the time, Pallas kernels for 0%

commit v1 on v0

v1 whole, which is shorter than its diff:
```python
import functools

import jax
import jax.numpy as jnp
from jax import lax
from jax.experimental import pallas as pl
from jax.experimental.pallas import tpu as pltpu
from jax.sharding import PartitionSpec as P

E = 192
HEADS = 6
HD = 32
HID = 768
F = 8
EPS = 1e-05
SCALE = HD ** (-0.5) * 1.4426950408889634
FAR = -1e30
MESH = pl.DeviceIdType.MESH
F32 = jnp.float32
BF16 = jnp.bfloat16

NX, NY, NZ, NC = 4, 4, 8, 2
TR, TE = 32, 16
RB = TR + TE
NQ = NZ * RB
KB = NZ * TR
HALF = KB // 2
STEPS = NX * NY

ORDER = [(0, 0), (1, 0), (2, 0), (0, 1), (0, 2), (3, 0), (1, 1), (2, 1),
         (1, 2), (2, 2), (0, 3), (3, 1), (3, 2), (1, 3), (2, 3), (3, 3)]
SLOT = {pos: i for i, pos in enumerate(ORDER)}


def nt(a, b):
    return lax.dot_general(a, b, (((1,), (1,)), ((), ())), preferred_element_type=F32)


def nn(a, b):
    return lax.dot_general(a, b, (((1,), (0,)), ((), ())), preferred_element_type=F32)


def norm(v):
    centred = v - jnp.mean(v, axis=-1, keepdims=True)
    spread = jnp.mean(centred * centred, axis=-1, keepdims=True)
    return centred * lax.rsqrt(spread + EPS)


def eye(n):
    r = lax.broadcasted_iota(jnp.int32, (n, n), 0)
    c = lax.broadcasted_iota(jnp.int32, (n, n), 1)
    return jnp.where(r == c, 1.0, 0.0).astype(BF16)


def head_mask(rows, h):
    lane = lax.broadcasted_iota(jnp.int32, (rows, E), 1)
    return (lane >= h * HD) & (lane < (h + 1) * HD)


def kernel(train_ref, test_ref, fw_ref, rw_ref, up_ref, down_ref,
           train_out, test_out,
           cell_tr, cell_te, x_ref, zs, zr, kbuf, qp, va, acc, mx, os_ref, or_ref, res,
           ex_send, ex_recv, z_send, z_recv, own_send, sib_send, ag_recv, ag_recv2, sib_recv,
           o_send, o_recv, loc):
    r = lax.axis_index("rows")
    h = lax.axis_index("feat")
    c = lax.rem(r, NC)
    z = lax.rem(r // NC, NZ)
    x = lax.rem(r // (NC * NZ), NX)
    ylo = r // (NC * NZ * NX)
    y = h * 2 + ylo

    def dev(x_, y_, z_, c_):
        row = ((lax.rem(y_, 2) * NX + x_) * NZ + z_) * NC + c_
        return {"rows": row, "feat": y_ // 2}

    first = jnp.where(c == 0, 1, 0)
    second = 1 - first

    def along(first_step, second_step):
        dx = first * first_step + second * second_step
        dy = second * first_step + first * second_step
        return dev(lax.rem(x + dx + NX, NX), lax.rem(y + dy + NY, NY), z, c)

    a_up, a_down = along(1, 0), along(-1, 0)
    b_up, b_down = along(0, 1), along(0, -1)
    sibling = dev(x, y, z, 1 - c)

    def z_line(d, other):
        return {"rows": ((ylo * NX + x) * NZ + lax.rem(z + d, NZ)) * NC + c,
                "feat": h if not other else 1 - h}

    barrier = pltpu.get_barrier_semaphore()
    for d in range(NZ):
        for other in (False, True):
            if d or other:
                pl.semaphore_signal(barrier, inc=1, device_id=z_line(d, other), device_id_type=MESH)
    for target in (a_up, a_down, b_up, b_down, sibling):
        pl.semaphore_signal(barrier, inc=1, device_id=target, device_id_type=MESH)
    pl.semaphore_wait(barrier, 2 * NZ - 1 + 5)

    def remote(src, dst, send, recv, target):
        return pltpu.make_async_remote_copy(src_ref=src, dst_ref=dst, send_sem=send, recv_sem=recv,
                                            device_id=target, device_id_type=MESH)

    partner = z_line(0, True)
    give_tr = pl.ds(pl.multiple_of((1 - h) * TR, TR), TR)
    give_te = pl.ds(pl.multiple_of((1 - h) * TE, TE), TE)
    ex = [remote(train_ref.at[give_tr], cell_tr.at[h], ex_send.at[0], ex_recv.at[0], partner),
          remote(test_ref.at[give_te], cell_te.at[h], ex_send.at[1], ex_recv.at[1], partner)]
    for copy in ex:
        copy.start()
    keep_tr = pl.ds(pl.multiple_of(h * TR, TR), TR)
    keep_te = pl.ds(pl.multiple_of(h * TE, TE), TE)
    cell_tr[h] = train_ref[keep_tr, :]
    cell_te[h] = test_ref[keep_te, :]
    for copy in ex:
        copy.wait()

    for f in range(F):
        lanes = slice((f % 4) * E, (f % 4 + 1) * E)
        for j in range(3):
            if j < 2:
                part = cell_tr[f // 4, 16 * j:16 * j + 16, lanes]
            else:
                part = cell_te[f // 4, :, lanes]
            x_ref[pl.ds(j * 128 + f * 16, 16), :] = part.astype(F32)
    cells = x_ref[...]
    n1 = norm(cells).astype(BF16)
    fq = nn(n1, fw_ref[0]).astype(BF16)
    fk = nn(n1, fw_ref[1]).astype(BF16)
    fv = nn(n1, fw_ref[2]).astype(BF16)
    same = (lax.rem(lax.broadcasted_iota(jnp.int32, (128, 128), 0), 16)
            == lax.rem(lax.broadcasted_iota(jnp.int32, (128, 128), 1), 16))
    zero = jnp.zeros((128, E), BF16)
    for j in range(3):
        rows = slice(128 * j, 128 * j + 128)
        qj, kj, vj = fq[rows], fk[rows], fv[rows]
        mixed = jnp.zeros((128, E), F32)
        for head in range(HEADS):
            mask = head_mask(128, head)
            s = nt(jnp.where(mask, qj, zero), kj) * SCALE
            s = jnp.where(same, s, FAR)
            w = jnp.exp2(s - jnp.max(s, axis=1, keepdims=True))
            total = jnp.sum(w, axis=1, keepdims=True)
            o = nn(w.astype(BF16), vj)
            mixed = jnp.where(mask, o / total, mixed)
        moved = nn(mixed.astype(BF16), fw_ref[3]).astype(BF16).astype(F32)
        after = (cells[rows] + moved).astype(BF16)
        for f in range(F):
            zs[f, 16 * j:16 * j + 16, :] = after[16 * f:16 * f + 16]

    z_copies = []
    for d in (4, 3, 5, 2, 6, 1, 7):
        copy = remote(zs.at[lax.rem(z + d, NZ)], zr.at[z], z_send.at[d], z_recv.at[d], z_line(d, False))
        copy.start()
        z_copies.append(copy)
    zr[z] = zs[z]
    for copy in z_copies:
        copy.wait_recv()

    a2 = zr[...].reshape(NQ, E).astype(F32)
    res[...] = a2
    n2 = norm(a2).astype(BF16)
    for k in range(NZ):
        kbuf[0, k * TR:(k + 1) * TR, :] = n2[k * RB:k * RB + TR]

    low, high = pl.ds(0, HALF), pl.ds(HALF, HALF)

    def send_block(slot, which, target, to_slot, rows, recv):
        src = kbuf.at[slot] if rows is None else kbuf.at[slot, rows]
        dst = kbuf.at[to_slot] if rows is None else kbuf.at[to_slot, rows]
        return remote(src, dst, own_send.at[slot, which], recv.at[to_slot], target)

    def sends(i):
        a, b = ORDER[i]
        out = []
        if (a, b) == (0, 0):
            out += [(0, a_up, SLOT[1, 0], None, ag_recv), (1, a_down, SLOT[2, 0], None, ag_recv)]
        if b == 0:
            out += [(2, b_up, SLOT[a, 1], None, ag_recv), (3, b_down, SLOT[a, 2], None, ag_recv)]
        if (a, b) == (1, 0):
            out += [(0, a_up, SLOT[3, 0], low, ag_recv)]
        if (a, b) == (2, 0):
            out += [(0, a_down, SLOT[3, 0], high, ag_recv2)]
        if b == 1:
            out += [(2, b_up, SLOT[a, 3], low, ag_recv)]
        if b == 2:
            out += [(2, b_down, SLOT[a, 3], high, ag_recv2)]
        return [send_block(i, *o) for o in out]

    def sib_copy(i):
        return remote(kbuf.at[i], kbuf.at[STEPS + i], sib_send.at[i], sib_recv.at[i], sibling)

    def handle(i):
        a, b = ORDER[i]
        if i:
            if a == 3 and b == 0 or b == 3:
                remote(kbuf.at[i, low], kbuf.at[i, low], own_send.at[i, 0], ag_recv.at[i], a_up).wait_recv()
                remote(kbuf.at[i, high], kbuf.at[i, high], own_send.at[i, 0], ag_recv2.at[i], a_up).wait_recv()
            else:
                remote(kbuf.at[i], kbuf.at[i], own_send.at[i, 0], ag_recv.at[i], a_up).wait_recv()
        for copy in sends(i):
            copy.start()
        sib_copy(i).start()

    handle(0)

    q2 = nn(n2, rw_ref[0]).astype(BF16)
    wk = rw_ref[1]
    zero = jnp.zeros((E, E), BF16)
    for head in range(HEADS):
        part = nt(jnp.where(head_mask(E, head), wk, zero), q2) * SCALE
        qp[head // 2, :, (head % 2) * NQ:(head % 2 + 1) * NQ] = part.astype(BF16)
    wvt = nt(eye(E), rw_ref[2]).astype(BF16)
    va[...] = jnp.ones_like(va)
    acc[...] = jnp.zeros_like(acc)
    mx[...] = jnp.full_like(mx, FAR)

    def step(i, carry):
        for k in range(1, STEPS):
            @pl.when(i == k - 1)
            def _():
                handle(k)
        remote(kbuf.at[0], kbuf.at[STEPS + i], sib_send.at[i], sib_recv.at[i], sibling).wait_recv()
        keys = jnp.concatenate([kbuf[i], kbuf[STEPS + i]], axis=0)
        vt = nt(wvt, keys).astype(BF16)
        for g in range(3):
            va[g, 0:64, :] = vt[64 * g:64 * g + 64]
        for g in range(3):
            s = nn(keys, qp[g])
            old = mx[g]
            new = jnp.maximum(old, jnp.max(s, axis=0, keepdims=True))
            mx[g] = new
            w = jnp.exp2(s - new).astype(BF16)
            acc[g] = acc[g] * jnp.exp2(old - new) + nn(va[g], w)
        return carry

    lax.fori_loop(0, STEPS, step, 0)

    parts = []
    for g in range(3):
        o = acc[g]
        o = o[0:64] / o[64:65]
        parts += [o[0:32, 0:NQ], o[32:64, NQ:2 * NQ]]
    mix_t = jnp.concatenate(parts, axis=0).astype(BF16)
    mix = nt(eye(NQ), mix_t).astype(BF16)
    after_row = res[...] + nn(mix, rw_ref[3])
    n3 = norm(after_row).astype(BF16)
    hidden = nn(n3, up_ref[...])
    hidden = (hidden * 0.5 * (1.0 + lax.erf(hidden * (2.0 ** -0.5)))).astype(BF16)
    out = (after_row + nn(hidden, down_ref[...])).astype(BF16)
    for k in range(NZ):
        os_ref[k] = out[k * RB:(k + 1) * RB]

    side = z // 4
    mine = lax.rem(z, 4)

    def out_copy(d):
        target = {"rows": ((ylo * NX + x) * NZ + lax.rem(z + d, NZ)) * NC + c, "feat": side}
        return remote(os_ref.at[lax.rem(z + d, NZ)], or_ref.at[mine, h], o_send.at[d], o_recv.at[mine, h], target)

    for d in (4, 3, 5, 2, 6, 1, 7):
        out_copy(d).start()

    @pl.when(side == h)
    def _():
        or_ref[mine, h] = os_ref[z]

    @pl.when(side != h)
    def _():
        out_copy(0).start()

    for i in range(4):
        for hs in range(2):
            own = (side == h) & (mine == i) & (h == hs)

            @pl.when(jnp.logical_not(own))
            def _():
                remote(os_ref.at[0], or_ref.at[i, hs], o_send.at[0], o_recv.at[i, hs], partner).wait_recv()

    for hs in range(2):
        blocks = [or_ref[i, hs] for i in range(4)]
        train_out[TR * hs:TR * hs + TR, :] = jnp.concatenate([b[0:TR] for b in blocks], axis=1)
        test_out[TE * hs:TE * hs + TE, :] = jnp.concatenate([b[TR:RB] for b in blocks], axis=1)

    for copy in z_copies:
        copy.wait_send()
    for i in range(STEPS):
        for copy in sends(i):
            copy.wait_send()
        sib_copy(i).wait_send()
    for d in range(1, NZ):
        out_copy(d).wait_send()

    @pl.when(side != h)
    def _():
        out_copy(0).wait_send()


def body(*args):
    train, test = args[0], args[1]
    dma = pltpu.SemaphoreType.DMA
    return pl.pallas_call(
        kernel,
        name="layer",
        out_shape=(jax.ShapeDtypeStruct(train.shape, BF16), jax.ShapeDtypeStruct(test.shape, BF16)),
        in_specs=[pl.BlockSpec(memory_space=pltpu.VMEM)] * 6,
        out_specs=(pl.BlockSpec(memory_space=pltpu.VMEM),) * 2,
        scratch_shapes=[
            pltpu.VMEM((2, TR, 4 * E), BF16),
            pltpu.VMEM((2, TE, 4 * E), BF16),
            pltpu.VMEM((NQ, E), F32),
            pltpu.VMEM((F, RB, E), BF16),
            pltpu.VMEM((NZ, RB, E), BF16),
            pltpu.VMEM((2 * STEPS, KB, E), BF16),
            pltpu.VMEM((3, E, 2 * NQ), BF16),
            pltpu.VMEM((3, 80, 2 * KB), BF16),
            pltpu.VMEM((3, 80, 2 * NQ), F32),
            pltpu.VMEM((3, 1, 2 * NQ), F32),
            pltpu.VMEM((NZ, RB, E), BF16),
            pltpu.VMEM((4, 2, RB, E), BF16),
            pltpu.VMEM((NQ, E), F32),
            dma((2,)), dma((2,)), dma((NZ,)), dma((NZ,)),
            dma((STEPS, 4)), dma((STEPS,)), dma((STEPS,)), dma((STEPS,)), dma((STEPS,)),
            dma((NZ,)), dma((4, 2)), dma((1,)),
        ],
        compiler_params=pltpu.CompilerParams(
            collective_id=0, has_side_effects=True, vmem_limit_bytes=60 * 1024 * 1024),
    )(*args)


def solution(mesh):
    return jax.shard_map(
        body,
        mesh=mesh,
        in_specs=(P("rows", "feat"), P("rows", "feat"), P(), P(), P(), P()),
        out_specs=(P("rows", "feat"), P("rows", "feat")),
        check_vma=False,
    )
```

time: 343 us -> 86.1 us (0.25)
  waiting for transfers between devices: 112 us -> 0 us
  Pallas kernels: 0 us -> 80.4 us
  matrix products: 78.5 us -> 0 us
  other arithmetic: 55.5 us -> 0 us
  local copies, waits for them, and re-layouts: 37.2 us -> 4.05 us
  blocking collectives: 29.2 us -> 0 us
  starting transfers between devices: 27.3 us -> 0 us
    all_to_all x3 -> x0, waiting for transfers between devices: 112 us -> none  [the longest x1 94.1 us: body(): lax.all_to_all(spread_copies(train_normed, copies), 'rows', split_axis=0,...]
    pallas_call x0 -> x1, Pallas kernels: none -> 80.4 us  [body(): pl.pallas_call(kernel, name='layer', out_shape=(jax.ShapeDtypeStruct(trai...]
    dot_general x41 -> x0, matrix products: 78.5 us -> none  [the longest x16 47.2 us: attend_block(): jnp.einsum('fkhd,qfhd->fhkq', key_block, queries, preferred_element_type=...]
    reduce_sum x22 -> x0, other arithmetic: 53.9 us -> none  [the longest x16 52.4 us: attend_block(): totals = totals * fading + jnp.sum(weights, axis=-2)]
    all_to_all x2 -> x0, blocking collectives: 29.2 us -> none  [the longest x1 21.9 us: body(): lax.all_to_all(mixed, 'rows', split_axis=0, concat_axis=0, tiled=True)]
    all_to_all x3 -> x0, starting transfers between devices: 27.3 us -> none  [the longest x1 15.6 us: body(): lax.all_to_all(query_pieces, 'rows', split_axis=0, concat_axis=0, tiled=T...]
    dynamic_slice x16 -> x0, local copies, waits for them, and re-layouts: 16.9 us -> none  [advance(): lax.dynamic_slice_in_dim(value_table, index * span, span, 1)]
    while x48 -> x0, local copies, waits for them, and re-layouts: 7.31 us -> none
  transfers between devices with their start and end apart: 3 -> 0, of which waited for: 3 -> 0; matrix products, arithmetic and copies ran while one was open for 0% -> 0% of each run, Pallas kernels for 0% -> 0%
where the time goes in v1:
time: 86.1 us; the launch traced here: 85.1 us
  Pallas kernels  80.4 us (93%)
  local copies, waits for them, and re-layouts  4.05 us (5%)
    pallas_call x1, Pallas kernels, body(): pl.pallas_call(kernel, name='layer', out_shape=(jax.ShapeDtypeStruct(trai...  80.4 us
    unnamed x5, local copies, waits for them, and re-layouts  4.05 us

profile of v1, /device:TPU:1, one launch (start us, length us, event | category | flops | bytes accessed | tf_op | source)
XLA Modules:
  0.0 85.1 jit_solution(16029792413963038774)
XLA Ops:
  0.6 1.9 %copy.8.down_ref = bf16[768,192]{1,0:T(8,128)(2,1)} copy(bf16[768,192]{0,1:T(8,128)(2,1)} %param.11) | data formatting | bytes 589824 | tf_op args[5]
  2.5 80.4 %layer.1 = (bf16[64,768]{1,0:T(8,128)(2,1)}, bf16[32,768]{1,0:T(8,128)(2,1)}) custom-call(bf16[64,768]{1,0:T(8,128)(2,1)} %train_ref.1, bf16[32,768]{1,0:T(8,128)(2,1)} %test_ref.1, bf16[4,192,192]{2,1,0:T(8,128)(2,1)} %fw_ref.1, bf16[4,192,192]{2,1,0:T(8,128)(2,1)} %rw_ref.1, bf16[192,768]{1,0:T(8,128)(2,1)} %up_ref.1, bf16[768,192]{1,0:T(8,128)(2,1)} %copy.8.down_ref), custom_call_target="tpu_custom_call" | custom-call | tf_op jit(solution)/shard_map/layer/pallas_call | solution.py:304
  82.9 0.0 copy-start
  83.0 1.6 %copy.11 = bf16[64,768]{1,0:T(8,128)(2,1)} copy(bf16[64,768]{1,0:T(8,128)(2,1)} %get-tuple-element.4) | data formatting | bytes 196608
  84.5 0.0 copy-done
  84.5 0.6 copy.12
Async XLA Ops:
  82.9 1.6 %copy-start = (bf16[32,768]{1,0:T(8,128)(2,1)S(1)}, bf16[32,768]{1,0:T(8,128)(2,1)}, u32[]{:S(2)}) copy-start(bf16[32,768]{1,0:T(8,128)(2,1)} %get-tuple-element.5) | copy-start | bytes 147460

commit v2 on v1

--- a/solution.py
+++ b/solution.py
@@ -26,6 +26,8 @@
 KB = NZ * TR
 HALF = KB // 2
 STEPS = NX * NY
+UW = 256
+UNITS = HEADS * NQ // UW
 
 ORDER = [(0, 0), (1, 0), (2, 0), (0, 1), (0, 2), (3, 0), (1, 1), (2, 1),
          (1, 2), (2, 2), (0, 3), (3, 1), (3, 2), (1, 3), (2, 3), (3, 3)]
@@ -59,7 +61,7 @@
 
 def kernel(train_ref, test_ref, fw_ref, rw_ref, up_ref, down_ref,
            train_out, test_out,
-           cell_tr, cell_te, x_ref, zs, zr, kbuf, qp, va, acc, mx, os_ref, or_ref, res,
+           cell_tr, cell_te, x_ref, zs, zr, kbuf, qp, va, sbuf, acc, m_acc, m_new, os_ref, or_ref, res,
            ex_send, ex_recv, z_send, z_recv, own_send, sib_send, ag_recv, ag_recv2, sib_recv,
            o_send, o_recv, loc):
     r = lax.axis_index("rows")
@@ -209,47 +211,87 @@
     q2 = nn(n2, rw_ref[0]).astype(BF16)
     wk = rw_ref[1]
     zero = jnp.zeros((E, E), BF16)
-    for head in range(HEADS):
-        part = nt(jnp.where(head_mask(E, head), wk, zero), q2) * SCALE
-        qp[head // 2, :, (head % 2) * NQ:(head % 2 + 1) * NQ] = part.astype(BF16)
+    for g in range(HEADS // 2):
+        pair = [(nt(jnp.where(head_mask(E, 2 * g + k), wk, zero), q2) * SCALE).astype(BF16) for k in range(2)]
+        pair = jnp.concatenate(pair, axis=1)
+        for t in range(3):
+            qp[3 * g + t] = pair[:, UW * t:UW * t + UW]
     wvt = nt(eye(E), rw_ref[2]).astype(BF16)
     va[...] = jnp.ones_like(va)
     acc[...] = jnp.zeros_like(acc)
-    mx[...] = jnp.full_like(mx, FAR)
+    m_acc[...] = jnp.full_like(m_acc, FAR)
+    m_new[...] = jnp.full_like(m_new, FAR)
+
+    span = [(0, 48), (0, 80), (32, 80)]
+
+    def score(i, u):
+        for k in range(2):
+            s = nn(kbuf[i + STEPS * k], qp[u])
+            sbuf[u % 3, KB * k:KB * k + KB, :] = s
+            m_new[u] = jnp.maximum(m_new[u], jnp.max(s, axis=0, keepdims=True))
+
+    def weigh(u):
+        lo, hi = span[u % 3]
+        new = m_new[u]
+        fade = jnp.exp2(m_acc[u] - new)
+        m_acc[u] = new
+        w = jnp.exp2(sbuf[u % 3] - new).astype(BF16)
+        acc[u, lo:hi, :] = acc[u, lo:hi, :] * fade + nn(va[u // 3, lo:hi, :], w)
+
+    def values(i):
+        for k in range(2):
+            vt = nt(wvt, kbuf[i + STEPS * k]).astype(BF16)
+            for g in range(3):
+                va[g, 0:32, KB * k:KB * k + KB] = vt[64 * g:64 * g + 32]
+                va[g, 48:80, KB * k:KB * k + KB] = vt[64 * g + 32:64 * g + 64]
+
+    def arrive(i):
+        remote(kbuf.at[0], kbuf.at[STEPS + i], sib_send.at[i], sib_recv.at[i], sibling).wait_recv()
+
+    def advance(i, following):
+        values(i)
+        for u in range(UNITS):
+            if u + 1 < UNITS:
+                score(i, u + 1)
+            elif following is not None:
+                score(following, 0)
+            weigh(u)
+
+    arrive(0)
+    score(0, 0)
+    advance(0, None)
+    handle(1)
+    arrive(1)
+    score(1, 0)
 
     def step(i, carry):
-        for k in range(1, STEPS):
+        for k in range(2, STEPS):
             @pl.when(i == k - 1)
             def _():
                 handle(k)
-        remote(kbuf.at[0], kbuf.at[STEPS + i], sib_send.at[i], sib_recv.at[i], sibling).wait_recv()
-        keys = jnp.concatenate([kbuf[i], kbuf[STEPS + i]], axis=0)
-        vt = nt(wvt, keys).astype(BF16)
-        for g in range(3):
-            va[g, 0:64, :] = vt[64 * g:64 * g + 64]
-        for g in range(3):
-            s = nn(keys, qp[g])
-            old = mx[g]
-            new = jnp.maximum(old, jnp.max(s, axis=0, keepdims=True))
-            mx[g] = new
-            w = jnp.exp2(s - new).astype(BF16)
-            acc[g] = acc[g] * jnp.exp2(old - new) + nn(va[g], w)
+
+        @pl.when(i < STEPS - 1)
+        def _():
+            arrive(i + 1)
+
+        advance(i, jnp.minimum(i + 1, STEPS - 1))
         return carry
 
-    lax.fori_loop(0, STEPS, step, 0)
+    lax.fori_loop(1, STEPS, step, 0)
 
     parts = []
     for g in range(3):
-        o = acc[g]
-        o = o[0:64] / o[64:65]
-        parts += [o[0:32, 0:NQ], o[32:64, NQ:2 * NQ]]
+        o = [acc[3 * g + t] for t in range(3)]
+        o = [v / v[32:33] for v in o]
+        parts += [jnp.concatenate([o[0][0:32], o[1][0:32, 0:UW // 2]], axis=1),
+                  jnp.concatenate([o[1][48:80, UW // 2:], o[2][48:80]], axis=1)]
     mix_t = jnp.concatenate(parts, axis=0).astype(BF16)
     mix = nt(eye(NQ), mix_t).astype(BF16)
     after_row = res[...] + nn(mix, rw_ref[3])
     n3 = norm(after_row).astype(BF16)
     hidden = nn(n3, up_ref[...])
     hidden = (hidden * 0.5 * (1.0 + lax.erf(hidden * (2.0 ** -0.5)))).astype(BF16)
-    out = (after_row + nn(hidden, down_ref[...])).astype(BF16)
+    out = (after_row + nt(hidden, down_ref[...])).astype(BF16)
     for k in range(NZ):
         os_ref[k] = out[k * RB:(k + 1) * RB]
 
@@ -314,10 +356,12 @@
             pltpu.VMEM((F, RB, E), BF16),
             pltpu.VMEM((NZ, RB, E), BF16),
             pltpu.VMEM((2 * STEPS, KB, E), BF16),
-            pltpu.VMEM((3, E, 2 * NQ), BF16),
+            pltpu.VMEM((UNITS, E, UW), BF16),
             pltpu.VMEM((3, 80, 2 * KB), BF16),
-            pltpu.VMEM((3, 80, 2 * NQ), F32),
-            pltpu.VMEM((3, 1, 2 * NQ), F32),
+            pltpu.VMEM((3, 2 * KB, UW), F32),
+            pltpu.VMEM((UNITS, 80, UW), F32),
+            pltpu.VMEM((UNITS, 1, UW), F32),
+            pltpu.VMEM((UNITS, 1, UW), F32),
             pltpu.VMEM((NZ, RB, E), BF16),
             pltpu.VMEM((4, 2, RB, E), BF16),
             pltpu.VMEM((NQ, E), F32),
@@ -327,7 +371,7 @@
         ],
         compiler_params=pltpu.CompilerParams(
             collective_id=0, has_side_effects=True, vmem_limit_bytes=60 * 1024 * 1024),
-    )(*args)
+    )(*args[:5], args[5].T)
 
 
 def solution(mesh):

time: 86.1 us -> 85.4 us (level)
  Pallas kernels: 80.4 us -> 82.4 us
  local copies, waits for them, and re-layouts: 4.05 us -> 2.18 us
    pallas_call x1, Pallas kernels: 80.4 us -> 82.4 us  [body(): pl.pallas_call(kernel, name='layer', out_shape=(jax.ShapeDtypeStruct(trai...]
    unnamed x5 -> x4, local copies, waits for them, and re-layouts: 4.05 us -> 2.18 us
where the time goes in v2:
time: 85.4 us; the launch traced here: 85.3 us
  Pallas kernels  82.4 us (96%)
  local copies, waits for them, and re-layouts  2.18 us (3%)
    pallas_call x1, Pallas kernels, body(): pl.pallas_call(kernel, name='layer', out_shape=(jax.ShapeDtypeStruct(trai...  82.4 us
    unnamed x4, local copies, waits for them, and re-layouts  2.18 us

profile of v2, /device:TPU:1, one launch (start us, length us, event | category | flops | bytes accessed | tf_op | source)
XLA Modules:
  0.0 85.3 jit_solution(15752878058248026728)
XLA Ops:
  0.6 82.4 %layer.1 = (bf16[64,768]{1,0:T(8,128)(2,1)}, bf16[32,768]{1,0:T(8,128)(2,1)}) custom-call(bf16[64,768]{1,0:T(8,128)(2,1)} %train_ref.1, bf16[32,768]{1,0:T(8,128)(2,1)} %test_ref.1, bf16[4,192,192]{2,1,0:T(8,128)(2,1)} %fw_ref.1, bf16[4,192,192]{2,1,0:T(8,128)(2,1)} %rw_ref.1, bf16[192,768]{1,0:T(8,128)(2,1)} %up_ref.1, bf16[192,768]{1,0:T(8,128)(2,1)} %bitcast.1), custom_call_target="tpu_custom_call" | custom-call | tf_op jit(solution)/shard_map/layer/pallas_call | solution.py:346
  83.1 0.0 copy-start
  83.1 1.6 %copy.10 = bf16[64,768]{1,0:T(8,128)(2,1)} copy(bf16[64,768]{1,0:T(8,128)(2,1)} %get-tuple-element.4) | data formatting | bytes 196608
  84.6 0.0 copy-done
  84.6 0.6 copy.11
Async XLA Ops:
  83.1 1.6 %copy-start = (bf16[32,768]{1,0:T(8,128)(2,1)S(1)}, bf16[32,768]{1,0:T(8,128)(2,1)}, u32[]{:S(2)}) copy-start(bf16[32,768]{1,0:T(8,128)(2,1)} %get-tuple-element.5) | copy-start | bytes 147460

commit v3 on v2

--- a/solution.py
+++ b/solution.py
@@ -24,7 +24,9 @@
 RB = TR + TE
 NQ = NZ * RB
 KB = NZ * TR
-HALF = KB // 2
+BLOCK = KB * 3 // 2
+HALF = BLOCK // 2
+ZB = RB + 2 * TE
 STEPS = NX * NY
 UW = 256
 UNITS = HEADS * NQ // UW
@@ -59,11 +61,12 @@
     return (lane >= h * HD) & (lane < (h + 1) * HD)
 
 
-def kernel(train_ref, test_ref, fw_ref, rw_ref, up_ref, down_ref,
+def kernel(train_in, test_in, fw_in, rw_in, up_in, down_in,
            train_out, test_out,
-           cell_tr, cell_te, x_ref, zs, zr, kbuf, qp, va, sbuf, acc, m_acc, m_new, os_ref, or_ref, res,
+           train_ref, test_ref, fw_ref, rw_ref, up_ref, down_ref,
+           cell_tr, cell_te, x_ref, zs, zr, kbuf, qp, wv, va, sbuf, acc, m_acc, m_new, os_ref, or_ref, res,
            ex_send, ex_recv, z_send, z_recv, own_send, sib_send, ag_recv, ag_recv2, sib_recv,
-           o_send, o_recv, loc):
+           o_send, o_recv, in_sem):
     r = lax.axis_index("rows")
     h = lax.axis_index("feat")
     c = lax.rem(r, NC)
@@ -99,6 +102,13 @@
                 pl.semaphore_signal(barrier, inc=1, device_id=z_line(d, other), device_id_type=MESH)
     for target in (a_up, a_down, b_up, b_down, sibling):
         pl.semaphore_signal(barrier, inc=1, device_id=target, device_id_type=MESH)
+    fetch = [pltpu.make_async_copy(a, b, in_sem.at[k]) for k, (a, b) in enumerate((
+        (train_in, train_ref), (test_in, test_ref), (fw_in, fw_ref), (rw_in, rw_ref),
+        (up_in, up_ref), (down_in, down_ref)))]
+    for copy in fetch:
+        copy.start()
+    fetch[0].wait()
+    fetch[1].wait()
     pl.semaphore_wait(barrier, 2 * NZ - 1 + 5)
 
     def remote(src, dst, send, recv, target):
@@ -116,6 +126,7 @@
     keep_te = pl.ds(pl.multiple_of(h * TE, TE), TE)
     cell_tr[h] = train_ref[keep_tr, :]
     cell_te[h] = test_ref[keep_te, :]
+    fetch[2].wait()
     for copy in ex:
         copy.wait()
 
@@ -135,6 +146,7 @@
     same = (lax.rem(lax.broadcasted_iota(jnp.int32, (128, 128), 0), 16)
             == lax.rem(lax.broadcasted_iota(jnp.int32, (128, 128), 1), 16))
     zero = jnp.zeros((128, E), BF16)
+    rest = []
     for j in range(3):
         rows = slice(128 * j, 128 * j + 128)
         qj, kj, vj = fq[rows], fk[rows], fv[rows]
@@ -150,7 +162,12 @@
         moved = nn(mixed.astype(BF16), fw_ref[3]).astype(BF16).astype(F32)
         after = (cells[rows] + moved).astype(BF16)
         for f in range(F):
-            zs[f, 16 * j:16 * j + 16, :] = after[16 * f:16 * f + 16]
+            zs[f, 16 * j:16 * j + 16, :] = after[16 * f:16 * f + 16, 0:128]
+        rest.append(after[:, 128:E])
+    for f in range(F):
+        own = slice(16 * f, 16 * f + 16)
+        zs[f, RB:RB + TE, :] = jnp.concatenate([rest[0][own], rest[1][own]], axis=1)
+        zs[f, RB + TE:ZB, :] = jnp.concatenate([rest[2][own], rest[2][own]], axis=1)
 
     z_copies = []
     for d in (4, 3, 5, 2, 6, 1, 7):
@@ -161,11 +178,15 @@
     for copy in z_copies:
         copy.wait_recv()
 
-    a2 = zr[...].reshape(NQ, E).astype(F32)
-    res[...] = a2
-    n2 = norm(a2).astype(BF16)
     for k in range(NZ):
-        kbuf[0, k * TR:(k + 1) * TR, :] = n2[k * RB:k * RB + TR]
+        left = zr[k, 0:RB, :]
+        pair = zr[k, RB:RB + TE, :]
+        right = jnp.concatenate([pair[:, 0:64], pair[:, 64:128], zr[k, RB + TE:ZB, 0:64]], axis=0)
+        res[k * RB:(k + 1) * RB, :] = jnp.concatenate([left, right], axis=1).astype(F32)
+    n2 = norm(res[...]).astype(BF16)
+    keys = jnp.concatenate([n2[k * RB:k * RB + TR] for k in range(NZ)], axis=0)
+    kbuf[0, 0:KB, :] = keys[:, 0:128]
+    kbuf[0, KB:BLOCK, :] = jnp.concatenate([keys[0:KB // 2, 128:E], keys[KB // 2:KB, 128:E]], axis=1)
 
     low, high = pl.ds(0, HALF), pl.ds(HALF, HALF)
 
@@ -208,6 +229,9 @@
 
     handle(0)
 
+    fetch[3].wait()
+    fetch[4].wait()
+    fetch[5].wait()
     q2 = nn(n2, rw_ref[0]).astype(BF16)
     wk = rw_ref[1]
     zero = jnp.zeros((E, E), BF16)
@@ -215,8 +239,15 @@
         pair = [(nt(jnp.where(head_mask(E, 2 * g + k), wk, zero), q2) * SCALE).astype(BF16) for k in range(2)]
         pair = jnp.concatenate(pair, axis=1)
         for t in range(3):
-            qp[3 * g + t] = pair[:, UW * t:UW * t + UW]
+            part = pair[:, UW * t:UW * t + UW]
+            for k in range(2):
+                qp[3 * g + t, k, 0:128, :] = part[0:128]
+                qp[3 * g + t, k, 128 + 64 * k:192 + 64 * k, :] = part[128:E]
+                qp[3 * g + t, k, 192 - 64 * k:256 - 64 * k, :] = jnp.zeros((64, UW), BF16)
     wvt = nt(eye(E), rw_ref[2]).astype(BF16)
+    gap = jnp.zeros((E, 64), BF16)
+    wv[0] = jnp.concatenate([wvt, gap], axis=1)
+    wv[1] = jnp.concatenate([wvt[:, 0:128], gap, wvt[:, 128:E]], axis=1)
     va[...] = jnp.ones_like(va)
     acc[...] = jnp.zeros_like(acc)
     m_acc[...] = jnp.full_like(m_acc, FAR)
@@ -224,9 +255,14 @@
 
     span = [(0, 48), (0, 80), (32, 80)]
 
+    def half_keys(i, k):
+        return jnp.concatenate([
+            jnp.concatenate([kbuf[i + STEPS * p, 128 * k:128 * k + 128, :], kbuf[i + STEPS * p, KB:BLOCK, :]], axis=1)
+            for p in range(2)], axis=0)
+
     def score(i, u):
         for k in range(2):
-            s = nn(kbuf[i + STEPS * k], qp[u])
+            s = nn(half_keys(i, k), qp[u, k])
             sbuf[u % 3, KB * k:KB * k + KB, :] = s
             m_new[u] = jnp.maximum(m_new[u], jnp.max(s, axis=0, keepdims=True))
 
@@ -240,7 +276,7 @@
 
     def values(i):
         for k in range(2):
-            vt = nt(wvt, kbuf[i + STEPS * k]).astype(BF16)
+            vt = nt(wv[k], half_keys(i, k)).astype(BF16)
             for g in range(3):
                 va[g, 0:32, KB * k:KB * k + KB] = vt[64 * g:64 * g + 32]
                 va[g, 48:80, KB * k:KB * k + KB] = vt[64 * g + 32:64 * g + 64]
@@ -261,12 +297,13 @@
     score(0, 0)
     advance(0, None)
     handle(1)
+    handle(2)
     arrive(1)
     score(1, 0)
 
     def step(i, carry):
-        for k in range(2, STEPS):
-            @pl.when(i == k - 1)
+        for k in range(3, STEPS):
+            @pl.when(i == k - 2)
             def _():
                 handle(k)
 
@@ -341,22 +378,24 @@
 
 
 def body(*args):
+    args = (*args[:5], args[5].T)
     train, test = args[0], args[1]
     dma = pltpu.SemaphoreType.DMA
     return pl.pallas_call(
         kernel,
         name="layer",
         out_shape=(jax.ShapeDtypeStruct(train.shape, BF16), jax.ShapeDtypeStruct(test.shape, BF16)),
-        in_specs=[pl.BlockSpec(memory_space=pltpu.VMEM)] * 6,
+        in_specs=[pl.BlockSpec(memory_space=pl.ANY)] * 6,
         out_specs=(pl.BlockSpec(memory_space=pltpu.VMEM),) * 2,
-        scratch_shapes=[
+        scratch_shapes=[pltpu.VMEM(v.shape, BF16) for v in args] + [
             pltpu.VMEM((2, TR, 4 * E), BF16),
             pltpu.VMEM((2, TE, 4 * E), BF16),
             pltpu.VMEM((NQ, E), F32),
-            pltpu.VMEM((F, RB, E), BF16),
-            pltpu.VMEM((NZ, RB, E), BF16),
-            pltpu.VMEM((2 * STEPS, KB, E), BF16),
-            pltpu.VMEM((UNITS, E, UW), BF16),
+            pltpu.VMEM((F, ZB, 128), BF16),
+            pltpu.VMEM((NZ, ZB, 128), BF16),
+            pltpu.VMEM((2 * STEPS, BLOCK, 128), BF16),
+            pltpu.VMEM((UNITS, 2, 256, UW), BF16),
+            pltpu.VMEM((2, E, 256), BF16),
             pltpu.VMEM((3, 80, 2 * KB), BF16),
             pltpu.VMEM((3, 2 * KB, UW), F32),
             pltpu.VMEM((UNITS, 80, UW), F32),
@@ -367,11 +406,11 @@
             pltpu.VMEM((NQ, E), F32),
             dma((2,)), dma((2,)), dma((NZ,)), dma((NZ,)),
             dma((STEPS, 4)), dma((STEPS,)), dma((STEPS,)), dma((STEPS,)), dma((STEPS,)),
-            dma((NZ,)), dma((4, 2)), dma((1,)),
+            dma((NZ,)), dma((4, 2)), dma((6,)),
         ],
         compiler_params=pltpu.CompilerParams(
             collective_id=0, has_side_effects=True, vmem_limit_bytes=60 * 1024 * 1024),
-    )(*args[:5], args[5].T)
+    )(*args)
 
 
 def solution(mesh):

time: 85.4 us -> 70.1 us (0.82)
  Pallas kernels: 82.4 us -> 67.1 us
    pallas_call x1, Pallas kernels: 82.4 us -> 67.1 us  [body(): pl.pallas_call(kernel, name='layer', out_shape=(jax.ShapeDtypeStruct(trai...]
where the time goes in v3:
time: 70.1 us; the launch traced here: 70 us
  Pallas kernels  67.1 us (96%)
  local copies, waits for them, and re-layouts  2.18 us (3%)
    pallas_call x1, Pallas kernels, body(): pl.pallas_call(kernel, name='layer', out_shape=(jax.ShapeDtypeStruct(trai...  67.1 us
    unnamed x4, local copies, waits for them, and re-layouts  2.18 us

profile of v3, /device:TPU:1, one launch (start us, length us, event | category | flops | bytes accessed | tf_op | source)
XLA Modules:
  0.0 70.0 jit_solution(14006958793179243400)
XLA Ops:
  0.6 67.1 %layer.1 = (bf16[64,768]{1,0:T(8,128)(2,1)}, bf16[32,768]{1,0:T(8,128)(2,1)}) custom-call(bf16[64,768]{1,0:T(8,128)(2,1)} %train_in.1, bf16[32,768]{1,0:T(8,128)(2,1)} %test_in.1, bf16[4,192,192]{2,1,0:T(8,128)(2,1)} %fw_in.1, bf16[4,192,192]{2,1,0:T(8,128)(2,1)} %rw_in.1, bf16[192,768]{1,0:T(8,128)(2,1)} %up_in.1, bf16[192,768]{1,0:T(8,128)(2,1)} %bitcast.1), custom_call_target="tpu_custom_call" | custom-call | tf_op jit(solution)/shard_map/layer/pallas_call | solution.py:384
  67.8 0.0 copy-start
  67.8 1.6 %copy.10 = bf16[64,768]{1,0:T(8,128)(2,1)} copy(bf16[64,768]{1,0:T(8,128)(2,1)} %get-tuple-element.4) | data formatting | bytes 196608
  69.3 0.0 copy-done
  69.3 0.6 copy.11
Async XLA Ops:
  67.8 1.6 %copy-start = (bf16[32,768]{1,0:T(8,128)(2,1)S(1)}, bf16[32,768]{1,0:T(8,128)(2,1)}, u32[]{:S(2)}) copy-start(bf16[32,768]{1,0:T(8,128)(2,1)} %get-tuple-element.5) | copy-start | bytes 147460

commit v4 on v3

--- a/solution.py
+++ b/solution.py
@@ -287,25 +287,32 @@
     def advance(i, following):
         values(i)
         for u in range(UNITS):
-            if u + 1 < UNITS:
-                score(i, u + 1)
+            if u + 2 < UNITS:
+                score(i, u + 2)
             elif following is not None:
-                score(following, 0)
+                score(following, u + 2 - UNITS)
             weigh(u)
 
     arrive(0)
     score(0, 0)
+    score(0, 1)
     advance(0, None)
     handle(1)
     handle(2)
     arrive(1)
     score(1, 0)
+    score(1, 1)
 
     def step(i, carry):
-        for k in range(3, STEPS):
-            @pl.when(i == k - 2)
-            def _():
-                handle(k)
+        def pick(lo, hi):
+            if hi - lo == 1:
+                handle(lo + 2)
+                return
+            mid = (lo + hi) // 2
+            pl.when(i < mid)(lambda: pick(lo, mid))
+            pl.when(i >= mid)(lambda: pick(mid, hi))
+
+        pl.when(i < STEPS - 2)(lambda: pick(1, STEPS - 2))
 
         @pl.when(i < STEPS - 1)
         def _():
@@ -384,7 +391,7 @@
     return pl.pallas_call(
         kernel,
         name="layer",
-        out_shape=(jax.ShapeDtypeStruct(train.shape, BF16), jax.ShapeDtypeStruct(test.shape, BF16)),
+        out_shape=(pltpu.VMEM(train.shape, BF16), pltpu.VMEM(test.shape, BF16)),
         in_specs=[pl.BlockSpec(memory_space=pl.ANY)] * 6,
         out_specs=(pl.BlockSpec(memory_space=pltpu.VMEM),) * 2,
         scratch_shapes=[pltpu.VMEM(v.shape, BF16) for v in args] + [

time: 70.1 us -> 61.4 us (0.88)
  Pallas kernels: 67.1 us -> 59.4 us
  local copies, waits for them, and re-layouts: 2.18 us -> 1.26 us
    pallas_call x1, Pallas kernels: 67.1 us -> 59.4 us  [body(): pl.pallas_call(kernel, name='layer', out_shape=(pltpu.VMEM(train.shape, B...]
    unnamed x4 -> x2, local copies, waits for them, and re-layouts: 2.18 us -> 1.26 us
where the time goes in v4:
time: 61.4 us; the launch traced here: 61.3 us
  Pallas kernels  59.4 us (97%)
  local copies, waits for them, and re-layouts  1.26 us (2%)
  between operations  0.64 us (1%)
    pallas_call x1, Pallas kernels, body(): pl.pallas_call(kernel, name='layer', out_shape=(pltpu.VMEM(train.shape, B...  59.4 us
    unnamed x2, local copies, waits for them, and re-layouts  1.26 us

profile of v4, /device:TPU:1, one launch (start us, length us, event | category | flops | bytes accessed | tf_op | source)
XLA Modules:
  0.0 61.3 jit_solution(7859549845282997804)
XLA Ops:
  0.6 59.4 %layer.1 = (bf16[64,768]{1,0:T(8,128)(2,1)S(1)}, bf16[32,768]{1,0:T(8,128)(2,1)S(1)}) custom-call(bf16[64,768]{1,0:T(8,128)(2,1)} %train_in.1, bf16[32,768]{1,0:T(8,128)(2,1)} %test_in.1, bf16[4,192,192]{2,1,0:T(8,128)(2,1)} %fw_in.1, bf16[4,192,192]{2,1,0:T(8,128)(2,1)} %rw_in.1, bf16[192,768]{1,0:T(8,128)(2,1)} %up_in.1, bf16[192,768]{1,0:T(8,128)(2,1)} %bitcast.1), custom_call_target="tpu_custom_call" | custom-call | tf_op jit(solution)/shard_map/layer/pallas_call | solution.py:391
  60.0 0.6 %copy.10 = bf16[64,768]{1,0:T(8,128)(2,1)} copy(bf16[64,768]{1,0:T(8,128)(2,1)S(1)} %get-tuple-element.2) | data formatting | bytes 196608
  60.6 0.6 %copy.11 = bf16[32,768]{1,0:T(8,128)(2,1)} copy(bf16[32,768]{1,0:T(8,128)(2,1)S(1)} %get-tuple-element.3) | data formatting | bytes 98304

commit v5 on v4

v5 whole, which is shorter than its diff:
```python
import functools

import jax
import jax.numpy as jnp
from jax import lax
from jax.experimental import pallas as pl
from jax.experimental.pallas import tpu as pltpu
from jax.sharding import PartitionSpec as P

E = 192
HEADS = 6
HD = 32
HID = 768
F = 8
EPS = 1e-05
SCALE = HD ** (-0.5) * 1.4426950408889634
FAR = -1e30
MESH = pl.DeviceIdType.MESH
F32 = jnp.float32
BF16 = jnp.bfloat16

NX, NY, NZ, NC = 4, 4, 8, 2
OWN = F // 2
TR, TE = 64, 32
RB = TR + TE
ZB = RB + RB // 2
NS = 4
NQ = NS * RB
KB = NS * TR
BLOCK = KB * 3 // 2
HALF = BLOCK // 2

ORDER = [(0, 0, 0), (0, 1, 0), (0, 0, 1), (0, 0, 2), (0, 1, 1), (0, 1, 2), (0, 0, 3), (0, 1, 3),
         (1, 0, 0), (1, 1, 0), (1, 0, 1), (1, 0, 2), (1, 1, 1), (1, 1, 2), (1, 0, 3), (1, 1, 3)]
SLOT = {pos: i for i, pos in enumerate(ORDER)}
STEPS = len(ORDER)
RELAY = 4
UW = 256
UNITS = HEADS * NQ // UW


def nt(a, b):
    return lax.dot_general(a, b, (((1,), (1,)), ((), ())), preferred_element_type=F32)


def nn(a, b):
    return lax.dot_general(a, b, (((1,), (0,)), ((), ())), preferred_element_type=F32)


def norm(v):
    centred = v - jnp.mean(v, axis=-1, keepdims=True)
    spread = jnp.mean(centred * centred, axis=-1, keepdims=True)
    return centred * lax.rsqrt(spread + EPS)


def eye(n):
    r = lax.broadcasted_iota(jnp.int32, (n, n), 0)
    c = lax.broadcasted_iota(jnp.int32, (n, n), 1)
    return jnp.where(r == c, 1.0, 0.0).astype(BF16)


def pack(ref, at, v):
    ref[at, 0:RB, :] = v[:, 0:128]
    for lo, n in ((0, TR // 2), (TR, TE // 2)):
        ref[at, RB + lo // 2:RB + lo // 2 + n, :] = jnp.concatenate(
            [v[lo:lo + n, 128:E], v[lo + n:lo + 2 * n, 128:E]], axis=1)


def unpack(ref, at):
    right = []
    for lo, n in ((0, TR // 2), (TR, TE // 2)):
        pair = ref[at, RB + lo // 2:RB + lo // 2 + n, :]
        right += [pair[:, 0:64], pair[:, 64:128]]
    return jnp.concatenate([ref[at, 0:RB, :], jnp.concatenate(right, axis=0)], axis=1)


def head_mask(rows, h):
    lane = lax.broadcasted_iota(jnp.int32, (rows, E), 1)
    return (lane >= h * HD) & (lane < (h + 1) * HD)


def kernel(train_in, test_in, fw_in, rw_in, up_in, down_in,
           train_out, test_out,
           train_ref, test_ref, fw_ref, rw_ref, up_ref, down_ref,
           cell_tr, cell_te, x_ref, x2_ref, zs, zr, kbuf, relay, qp, wv, va, sbuf, acc, m_acc, m_new, os_ref, or_ref, res,
           ex_send, ex_recv, z_send, z_recv, own_send, sib_send, ag_recv, ag_recv2, sib_recv,
           o_send, o_recv, rel_send, rel_recv, in_sem):
    r = lax.axis_index("rows")
    h = lax.axis_index("feat")
    c = lax.rem(r, NC)
    z = lax.rem(r // NC, NZ)
    x = lax.rem(r // (NC * NZ), NX)
    ylo = r // (NC * NZ * NX)
    y = h * 2 + ylo

    def dev(x_, y_, z_, c_):
        row = ((lax.rem(y_, 2) * NX + x_) * NZ + z_) * NC + c_
        return {"rows": row, "feat": y_ // 2}

    def dz(d):
        return dev(x, y, lax.rem(z + d + NZ, NZ), c)

    x_up, x_down = dev(lax.rem(x + 1, NX), y, z, c), dev(lax.rem(x + 3, NX), y, z, c)
    y_pair = dev(x, 2 * h + 1 - ylo, z, c)
    sibling = dev(x, y, z, 1 - c)
    partner = dev(x, lax.rem(y + 2, NY), z, c)
    two = jnp.where(lax.rem(z, 2) == 0, 2, -2)
    hop = jnp.where(c == 0, 2, -2)

    barrier = pltpu.get_barrier_semaphore()
    peers = (partner, dz(2), dz(-2), dz(1), dz(-1), x_up, x_down, y_pair, sibling)
    for target in peers:
        pl.semaphore_signal(barrier, inc=1, device_id=target, device_id_type=MESH)
    fetch = [pltpu.make_async_copy(a, b, in_sem.at[k]) for k, (a, b) in enumerate((
        (train_in, train_ref), (test_in, test_ref), (fw_in, fw_ref), (rw_in, rw_ref),
        (up_in, up_ref), (down_in, down_ref)))]
    for copy in fetch:
        copy.start()
    fetch[0].wait()
    fetch[1].wait()
    pl.semaphore_wait(barrier, len(peers))

    def remote(src, dst, send, recv, target):
        return pltpu.make_async_remote_copy(src_ref=src, dst_ref=dst, send_sem=send, recv_sem=recv,
                                            device_id=target, device_id_type=MESH)

    ex = [remote(train_ref, cell_tr, ex_send.at[0], ex_recv.at[0], partner),
          remote(test_ref, cell_te, ex_send.at[1], ex_recv.at[1], partner)]
    for copy in ex:
        copy.start()

    def gather(tr, te, to):
        for f in range(OWN):
            for j in range(RB // 16):
                ref, row = (tr, 16 * j) if j < TR // 16 else (te, 16 * j - TR)
                to[64 * j + 16 * f:64 * j + 16 * f + 16, :] = ref[row:row + 16, f * E:(f + 1) * E].astype(F32)

    gather(train_ref, test_ref, x_ref)
    n1 = norm(x_ref[...]).astype(BF16)
    fetch[2].wait()
    fq = nn(n1, fw_ref[0]).astype(BF16)
    fk = nn(n1, fw_ref[1]).astype(BF16)
    fv = nn(n1, fw_ref[2]).astype(BF16)
    for copy in ex:
        copy.wait_recv()
    gather(cell_tr, cell_te, x2_ref)
    n1 = norm(x2_ref[...]).astype(BF16)
    ok = nn(n1, fw_ref[1]).astype(BF16)
    ov = nn(n1, fw_ref[2]).astype(BF16)
    shape = (HEADS * 64, 128)
    same = (lax.rem(lax.broadcasted_iota(jnp.int32, shape, 0), 16)
            == lax.rem(lax.broadcasted_iota(jnp.int32, shape, 1), 16))
    masks = [head_mask(64, head) for head in range(HEADS)]
    zero = jnp.zeros((64, E), BF16)
    mixes = []
    for j in range(RB // 16):
        rows = slice(64 * j, 64 * j + 64)
        qj = fq[rows]
        kj = jnp.concatenate([fk[rows], ok[rows]], axis=0)
        vj = jnp.concatenate([fv[rows], ov[rows]], axis=0)
        s = nt(jnp.concatenate([jnp.where(m, qj, zero) for m in masks], axis=0), kj) * SCALE
        s = jnp.where(same, s, FAR)
        w = jnp.exp2(s - jnp.max(s, axis=1, keepdims=True))
        o = nn(w.astype(BF16), vj) / jnp.sum(w, axis=1, keepdims=True)
        mixed = o[0:64]
        for head in range(1, HEADS):
            mixed = jnp.where(masks[head], o[64 * head:64 * head + 64], mixed)
        mixes.append(mixed.astype(BF16))
    moved = nn(jnp.concatenate(mixes, axis=0), fw_ref[3]).astype(BF16).astype(F32)
    after = (x_ref[...] + moved).astype(BF16)

    for f in range(OWN):
        pack(zs, f, jnp.concatenate([after[64 * j + 16 * f:64 * j + 16 * f + 16] for j in range(RB // 16)], axis=0))
    z_copies = [remote(zs.at[lax.rem(z + d + NZ, OWN)], zr.at[slot], z_send.at[slot], z_recv.at[slot], dz(d))
                for slot, d in ((3, two), (1, 1), (2, -1))]
    for copy in z_copies:
        copy.start()
    zr[0] = zs[lax.rem(z, OWN)]
    for copy in z_copies:
        copy.wait_recv()

    for k in range(NS):
        res[k * RB:(k + 1) * RB, :] = unpack(zr, k).astype(F32)
    n2 = norm(res[...]).astype(BF16)
    keys = jnp.concatenate([n2[k * RB:k * RB + TR] for k in range(NS)], axis=0)
    kbuf[0, 0:KB, :] = keys[:, 0:128]
    kbuf[0, KB:BLOCK, :] = jnp.concatenate([keys[0:KB // 2, 128:E], keys[KB // 2:KB, 128:E]], axis=1)

    low, high = pl.ds(0, HALF), pl.ds(HALF, HALF)

    def send_block(slot, which, target, to_slot, rows, recv):
        src = kbuf.at[slot] if rows is None else kbuf.at[slot, rows]
        dst = kbuf.at[to_slot] if rows is None else kbuf.at[to_slot, rows]
        return remote(src, dst, own_send.at[slot, which], recv.at[to_slot], target)

    def sends(i):
        t, p, a = ORDER[i]
        out = []
        if (p, a) == (0, 0):
            out += [(2, y_pair, SLOT[t, 1, 0], None, ag_recv)]
        if a == 0:
            out += [(0, x_up, SLOT[t, p, 1], None, ag_recv), (1, x_down, SLOT[t, p, 2], None, ag_recv)]
        if a == 1:
            out += [(0, x_up, SLOT[t, p, 3], low, ag_recv)]
        if a == 2:
            out += [(1, x_down, SLOT[t, p, 3], high, ag_recv2)]
        return [send_block(i, *o) for o in out]

    def sib_copy(i):
        return remote(kbuf.at[i], kbuf.at[STEPS + i], sib_send.at[i], sib_recv.at[i], sibling)

    via = remote(kbuf.at[0], relay, rel_send.at[0], rel_recv.at[0], dz(hop))
    onward = remote(relay, kbuf.at[SLOT[1, 0, 0]], rel_send.at[1], ag_recv.at[SLOT[1, 0, 0]], dz(hop))

    def handle(i):
        t, p, a = ORDER[i]
        if i:
            if a == 3:
                remote(kbuf.at[i, low], kbuf.at[i, low], own_send.at[i, 0], ag_recv.at[i], x_up).wait_recv()
                remote(kbuf.at[i, high], kbuf.at[i, high], own_send.at[i, 0], ag_recv2.at[i], x_up).wait_recv()
            else:
                remote(kbuf.at[i], kbuf.at[i], own_send.at[i, 0], ag_recv.at[i], x_up).wait_recv()
        for copy in sends(i):
            copy.start()
        sib_copy(i).start()

    via.start()
    handle(0)

    fetch[3].wait()
    fetch[4].wait()
    fetch[5].wait()
    q2 = nn(n2, rw_ref[0]).astype(BF16)
    wk = rw_ref[1]
    zero = jnp.zeros((E, E), BF16)
    for g in range(HEADS // 2):
        pair = [(nt(jnp.where(head_mask(E, 2 * g + k), wk, zero), q2) * SCALE).astype(BF16) for k in range(2)]
        pair = jnp.concatenate(pair, axis=1)
        for t in range(3):
            part = pair[:, UW * t:UW * t + UW]
            for k in range(2):
                qp[3 * g + t, k, 0:128, :] = part[0:128]
                qp[3 * g + t, k, 128 + 64 * k:192 + 64 * k, :] = part[128:E]
                qp[3 * g + t, k, 192 - 64 * k:256 - 64 * k, :] = jnp.zeros((64, UW), BF16)
    wvt = nt(eye(E), rw_ref[2]).astype(BF16)
    gap = jnp.zeros((E, 64), BF16)
    wv[0] = jnp.concatenate([wvt, gap], axis=1)
    wv[1] = jnp.concatenate([wvt[:, 0:128], gap, wvt[:, 128:E]], axis=1)
    va[...] = jnp.ones_like(va)
    acc[...] = jnp.zeros_like(acc)
    m_acc[...] = jnp.full_like(m_acc, FAR)
    m_new[...] = jnp.full_like(m_new, FAR)

    span = [(0, 48), (0, 80), (32, 80)]

    def half_keys(i, k):
        return jnp.concatenate([
            jnp.concatenate([kbuf[i + STEPS * p, 128 * k:128 * k + 128, :], kbuf[i + STEPS * p, KB:BLOCK, :]], axis=1)
            for p in range(2)], axis=0)

    def score(i, u):
        for k in range(2):
            s = nn(half_keys(i, k), qp[u, k])
            sbuf[u % 3, KB * k:KB * k + KB, :] = s
            m_new[u] = jnp.maximum(m_new[u], jnp.max(s, axis=0, keepdims=True))

    def weigh(u):
        lo, hi = span[u % 3]
        new = m_new[u]
        fade = jnp.exp2(m_acc[u] - new)
        m_acc[u] = new
        w = jnp.exp2(sbuf[u % 3] - new).astype(BF16)
        acc[u, lo:hi, :] = acc[u, lo:hi, :] * fade + nn(va[u // 3, lo:hi, :], w)

    def values(i):
        for k in range(2):
            vt = nt(wv[k], half_keys(i, k)).astype(BF16)
            for g in range(3):
                va[g, 0:32, KB * k:KB * k + KB] = vt[64 * g:64 * g + 32]
                va[g, 48:80, KB * k:KB * k + KB] = vt[64 * g + 32:64 * g + 64]

    def arrive(i):
        remote(kbuf.at[0], kbuf.at[STEPS + i], sib_send.at[i], sib_recv.at[i], sibling).wait_recv()

    def advance(i, following):
        values(i)
        for u in range(UNITS):
            if u + 2 < UNITS:
                score(i, u + 2)
            elif following is not None:
                score(following, u + 2 - UNITS)
            weigh(u)

    arrive(0)
    score(0, 0)
    score(0, 1)
    advance(0, None)
    handle(1)
    handle(2)
    arrive(1)
    score(1, 0)
    score(1, 1)

    def step(i, carry):
        def pick(lo, hi):
            if hi - lo == 1:
                if lo + 2 == RELAY:
                    via.wait_recv()
                    onward.start()
                handle(lo + 2)
                return
            mid = (lo + hi) // 2
            pl.when(i < mid)(lambda: pick(lo, mid))
            pl.when(i >= mid)(lambda: pick(mid, hi))

        pl.when(i < STEPS - 2)(lambda: pick(1, STEPS - 2))

        @pl.when(i < STEPS - 1)
        def _():
            arrive(i + 1)

        advance(i, jnp.minimum(i + 1, STEPS - 1))
        return carry

    lax.fori_loop(1, STEPS, step, 0)

    parts = []
    for g in range(3):
        o = [acc[3 * g + t] for t in range(3)]
        o = [v / v[32:33] for v in o]
        parts += [jnp.concatenate([o[0][0:32], o[1][0:32, 0:UW // 2]], axis=1),
                  jnp.concatenate([o[1][48:80, UW // 2:], o[2][48:80]], axis=1)]
    mix_t = jnp.concatenate(parts, axis=0).astype(BF16)
    mix = nt(eye(NQ), mix_t).astype(BF16)
    after_row = res[...] + nn(mix, rw_ref[3])
    n3 = norm(after_row).astype(BF16)
    hidden = nn(n3, up_ref[...])
    hidden = (hidden * 0.5 * (1.0 + lax.erf(hidden * (2.0 ** -0.5)))).astype(BF16)
    out = (after_row + nt(hidden, down_ref[...])).astype(BF16)
    for k in range(NS):
        pack(os_ref, k, out[k * RB:(k + 1) * RB])

    mine = lax.rem(z, OWN)
    o_copies = [remote(os_ref.at[slot], or_ref.at[mine], o_send.at[slot], o_recv.at[mine], dz(d))
                for slot, d in ((3, -two), (1, -1), (2, 1))]
    for copy in o_copies:
        copy.start()
    or_ref[mine] = os_ref[0]
    for d in (1, -1, 2):
        f = lax.rem(z + d + NZ, OWN)
        remote(os_ref.at[0], or_ref.at[f], o_send.at[0], o_recv.at[f], sibling).wait_recv()
    blocks = [unpack(or_ref, f) for f in range(OWN)]
    train_out[...] = jnp.concatenate([v[0:TR] for v in blocks], axis=1)
    test_out[...] = jnp.concatenate([v[TR:RB] for v in blocks], axis=1)

    for copy in ex + z_copies + o_copies + [via, onward]:
        copy.wait_send()
    for i in range(STEPS):
        for copy in sends(i):
            copy.wait_send()
        sib_copy(i).wait_send()


def body(*args):
    args = (*args[:5], args[5].T)
    train, test = args[0], args[1]
    dma = pltpu.SemaphoreType.DMA
    return pl.pallas_call(
        kernel,
        name="layer",
        out_shape=(pltpu.VMEM(train.shape, BF16), pltpu.VMEM(test.shape, BF16)),
        in_specs=[pl.BlockSpec(memory_space=pl.ANY)] * 6,
        out_specs=(pl.BlockSpec(memory_space=pltpu.VMEM),) * 2,
        scratch_shapes=[pltpu.VMEM(v.shape, BF16) for v in args] + [
            pltpu.VMEM((TR, OWN * E), BF16),
            pltpu.VMEM((TE, OWN * E), BF16),
            pltpu.VMEM((OWN * RB, E), F32),
            pltpu.VMEM((OWN * RB, E), F32),
            pltpu.VMEM((OWN, ZB, 128), BF16),
            pltpu.VMEM((NS, ZB, 128), BF16),
            pltpu.VMEM((2 * STEPS, BLOCK, 128), BF16),
            pltpu.VMEM((BLOCK, 128), BF16),
            pltpu.VMEM((UNITS, 2, 256, UW), BF16),
            pltpu.VMEM((2, E, 256), BF16),
            pltpu.VMEM((3, 80, 2 * KB), BF16),
            pltpu.VMEM((3, 2 * KB, UW), F32),
            pltpu.VMEM((UNITS, 80, UW), F32),
            pltpu.VMEM((UNITS, 1, UW), F32),
            pltpu.VMEM((UNITS, 1, UW), F32),
            pltpu.VMEM((NS, ZB, 128), BF16),
            pltpu.VMEM((OWN, ZB, 128), BF16),
            pltpu.VMEM((NQ, E), F32),
            dma((2,)), dma((2,)), dma((NS,)), dma((NS,)),
            dma((STEPS, 4)), dma((STEPS,)), dma((STEPS,)), dma((STEPS,)), dma((STEPS,)),
            dma((NS,)), dma((OWN,)), dma((2,)), dma((1,)), dma((6,)),
        ],
        compiler_params=pltpu.CompilerParams(
            collective_id=0, has_side_effects=True, vmem_limit_bytes=60 * 1024 * 1024),
    )(*args)


def solution(mesh):
    return jax.shard_map(
        body,
        mesh=mesh,
        in_specs=(P("rows", "feat"), P("rows", "feat"), P(), P(), P(), P()),
        out_specs=(P("rows", "feat"), P("rows", "feat")),
        check_vma=False,
    )
```

time: 61.4 us -> 59.3 us (0.966)
  Pallas kernels: 59.4 us -> 57.3 us
    pallas_call x1, Pallas kernels: 59.4 us -> 57.3 us  [body(): pl.pallas_call(kernel, name='layer', out_shape=(pltpu.VMEM(train.shape, B...]
where the time goes in v5:
time: 59.3 us; the launch traced here: 59.2 us
  Pallas kernels  57.3 us (97%)
  local copies, waits for them, and re-layouts  1.26 us (2%)
  between operations  0.64 us (1%)
    pallas_call x1, Pallas kernels, body(): pl.pallas_call(kernel, name='layer', out_shape=(pltpu.VMEM(train.shape, B...  57.3 us
    unnamed x2, local copies, waits for them, and re-layouts  1.26 us

profile of v5, /device:TPU:1, one launch (start us, length us, event | category | flops | bytes accessed | tf_op | source)
XLA Modules:
  0.0 59.2 jit_solution(14678974389118441696)
XLA Ops:
  0.6 57.3 %layer.1 = (bf16[64,768]{1,0:T(8,128)(2,1)S(1)}, bf16[32,768]{1,0:T(8,128)(2,1)S(1)}) custom-call(bf16[64,768]{1,0:T(8,128)(2,1)} %train_in.1, bf16[32,768]{1,0:T(8,128)(2,1)} %test_in.1, bf16[4,192,192]{2,1,0:T(8,128)(2,1)} %fw_in.1, bf16[4,192,192]{2,1,0:T(8,128)(2,1)} %rw_in.1, bf16[192,768]{1,0:T(8,128)(2,1)} %up_in.1, bf16[192,768]{1,0:T(8,128)(2,1)} %bitcast.1), custom_call_target="tpu_custom_call" | custom-call | tf_op jit(solution)/shard_map/layer/pallas_call | solution.py:368
  57.9 0.6 %copy.10 = bf16[64,768]{1,0:T(8,128)(2,1)} copy(bf16[64,768]{1,0:T(8,128)(2,1)S(1)} %get-tuple-element.2) | data formatting | bytes 196608
  58.6 0.6 %copy.11 = bf16[32,768]{1,0:T(8,128)(2,1)} copy(bf16[32,768]{1,0:T(8,128)(2,1)S(1)} %get-tuple-element.3) | data formatting | bytes 98304

commit v6 on v5

--- a/solution.py
+++ b/solution.py
@@ -24,17 +24,20 @@
 TR, TE = 64, 32
 RB = TR + TE
 ZB = RB + RB // 2
+PR = 32
+PB = PR + PR // 2
+PIECES = RB // PR
 NS = 4
 NQ = NS * RB
 KB = NS * TR
 BLOCK = KB * 3 // 2
 HALF = BLOCK // 2
 
-ORDER = [(0, 0, 0), (0, 1, 0), (0, 0, 1), (0, 0, 2), (0, 1, 1), (0, 1, 2), (0, 0, 3), (0, 1, 3),
-         (1, 0, 0), (1, 1, 0), (1, 0, 1), (1, 0, 2), (1, 1, 1), (1, 1, 2), (1, 0, 3), (1, 1, 3)]
+ORDER = [(0, 0, 0), (0, 1, 0), (0, 0, 1), (0, 0, 2), (0, 1, 1), (0, 1, 2), (1, 0, 0), (0, 0, 3),
+         (0, 1, 3), (1, 1, 0), (1, 0, 1), (1, 0, 2), (1, 1, 1), (1, 1, 2), (1, 0, 3), (1, 1, 3)]
 SLOT = {pos: i for i, pos in enumerate(ORDER)}
 STEPS = len(ORDER)
-RELAY = 4
+RELAY = 3
 UW = 256
 UNITS = HEADS * NQ // UW
 
@@ -59,19 +62,18 @@
     return jnp.where(r == c, 1.0, 0.0).astype(BF16)
 
 
-def pack(ref, at, v):
-    ref[at, 0:RB, :] = v[:, 0:128]
-    for lo, n in ((0, TR // 2), (TR, TE // 2)):
-        ref[at, RB + lo // 2:RB + lo // 2 + n, :] = jnp.concatenate(
-            [v[lo:lo + n, 128:E], v[lo + n:lo + 2 * n, 128:E]], axis=1)
+def pack_piece(ref, at, q, v):
+    ref[at, q * PB:q * PB + PR, :] = v[:, 0:128]
+    ref[at, q * PB + PR:(q + 1) * PB, :] = jnp.concatenate([v[0:PR // 2, 128:E], v[PR // 2:PR, 128:E]], axis=1)
 
 
 def unpack(ref, at):
-    right = []
-    for lo, n in ((0, TR // 2), (TR, TE // 2)):
-        pair = ref[at, RB + lo // 2:RB + lo // 2 + n, :]
-        right += [pair[:, 0:64], pair[:, 64:128]]
-    return jnp.concatenate([ref[at, 0:RB, :], jnp.concatenate(right, axis=0)], axis=1)
+    out = []
+    for q in range(RB // PR):
+        pair = ref[at, q * PB + PR:(q + 1) * PB, :]
+        right = jnp.concatenate([pair[:, 0:64], pair[:, 64:128]], axis=0)
+        out.append(jnp.concatenate([ref[at, q * PB:q * PB + PR, :], right], axis=1))
+    return jnp.concatenate(out, axis=0)
 
 
 def head_mask(rows, h):
@@ -82,7 +84,7 @@
 def kernel(train_in, test_in, fw_in, rw_in, up_in, down_in,
            train_out, test_out,
            train_ref, test_ref, fw_ref, rw_ref, up_ref, down_ref,
-           cell_tr, cell_te, x_ref, x2_ref, zs, zr, kbuf, relay, qp, wv, va, sbuf, acc, m_acc, m_new, os_ref, or_ref, res,
+           cell_tr, cell_te, x_ref, zs, zr, kbuf, relay, qp, wv, va, sbuf, acc, m_acc, m_new, os_ref, or_ref, res,
            ex_send, ex_recv, z_send, z_recv, own_send, sib_send, ag_recv, ag_recv2, sib_recv,
            o_send, o_recv, rel_send, rel_recv, in_sem):
     r = lax.axis_index("rows")
@@ -101,14 +103,16 @@
         return dev(x, y, lax.rem(z + d + NZ, NZ), c)
 
     x_up, x_down = dev(lax.rem(x + 1, NX), y, z, c), dev(lax.rem(x + 3, NX), y, z, c)
-    y_pair = dev(x, 2 * h + 1 - ylo, z, c)
+    y_other = 2 * h + 1 - ylo
+    y_pair = dev(x, y_other, z, c)
+    d_up, d_down = dev(lax.rem(x + 1, NX), y_other, z, c), dev(lax.rem(x + 3, NX), y_other, z, c)
     sibling = dev(x, y, z, 1 - c)
     partner = dev(x, lax.rem(y + 2, NY), z, c)
     two = jnp.where(lax.rem(z, 2) == 0, 2, -2)
     hop = jnp.where(c == 0, 2, -2)
 
     barrier = pltpu.get_barrier_semaphore()
-    peers = (partner, dz(2), dz(-2), dz(1), dz(-1), x_up, x_down, y_pair, sibling)
+    peers = (partner, dz(2), dz(-2), d_up, d_down, dz(1), dz(-1), x_up, x_down, y_pair, sibling)
     for target in peers:
         pl.semaphore_signal(barrier, inc=1, device_id=target, device_id_type=MESH)
     fetch = [pltpu.make_async_copy(a, b, in_sem.at[k]) for k, (a, b) in enumerate((
@@ -124,57 +128,59 @@
         return pltpu.make_async_remote_copy(src_ref=src, dst_ref=dst, send_sem=send, recv_sem=recv,
                                             device_id=target, device_id_type=MESH)
 
-    ex = [remote(train_ref, cell_tr, ex_send.at[0], ex_recv.at[0], partner),
-          remote(test_ref, cell_te, ex_send.at[1], ex_recv.at[1], partner)]
+    spots = [(train_ref, cell_tr, 0), (train_ref, cell_tr, PR), (test_ref, cell_te, 0)]
+    ex = [remote(src.at[pl.ds(at, PR)], dst.at[pl.ds(at, PR)], ex_send.at[q], ex_recv.at[q], partner)
+          for q, (src, dst, at) in enumerate(spots)]
     for copy in ex:
         copy.start()
 
-    def gather(tr, te, to):
-        for f in range(OWN):
-            for j in range(RB // 16):
-                ref, row = (tr, 16 * j) if j < TR // 16 else (te, 16 * j - TR)
-                to[64 * j + 16 * f:64 * j + 16 * f + 16, :] = ref[row:row + 16, f * E:(f + 1) * E].astype(F32)
-
-    gather(train_ref, test_ref, x_ref)
-    n1 = norm(x_ref[...]).astype(BF16)
-    fetch[2].wait()
-    fq = nn(n1, fw_ref[0]).astype(BF16)
-    fk = nn(n1, fw_ref[1]).astype(BF16)
-    fv = nn(n1, fw_ref[2]).astype(BF16)
-    for copy in ex:
-        copy.wait_recv()
-    gather(cell_tr, cell_te, x2_ref)
-    n1 = norm(x2_ref[...]).astype(BF16)
-    ok = nn(n1, fw_ref[1]).astype(BF16)
-    ov = nn(n1, fw_ref[2]).astype(BF16)
+    def gather(ref, at):
+        return jnp.concatenate([ref[at + 16 * j:at + 16 * j + 16, f * E:(f + 1) * E]
+                                for j in range(PR // 16) for f in range(OWN)], axis=0).astype(F32)
+
     shape = (HEADS * 64, 128)
     same = (lax.rem(lax.broadcasted_iota(jnp.int32, shape, 0), 16)
             == lax.rem(lax.broadcasted_iota(jnp.int32, shape, 1), 16))
     masks = [head_mask(64, head) for head in range(HEADS)]
     zero = jnp.zeros((64, E), BF16)
-    mixes = []
-    for j in range(RB // 16):
-        rows = slice(64 * j, 64 * j + 64)
-        qj = fq[rows]
-        kj = jnp.concatenate([fk[rows], ok[rows]], axis=0)
-        vj = jnp.concatenate([fv[rows], ov[rows]], axis=0)
-        s = nt(jnp.concatenate([jnp.where(m, qj, zero) for m in masks], axis=0), kj) * SCALE
-        s = jnp.where(same, s, FAR)
-        w = jnp.exp2(s - jnp.max(s, axis=1, keepdims=True))
-        o = nn(w.astype(BF16), vj) / jnp.sum(w, axis=1, keepdims=True)
-        mixed = o[0:64]
-        for head in range(1, HEADS):
-            mixed = jnp.where(masks[head], o[64 * head:64 * head + 64], mixed)
-        mixes.append(mixed.astype(BF16))
-    moved = nn(jnp.concatenate(mixes, axis=0), fw_ref[3]).astype(BF16).astype(F32)
-    after = (x_ref[...] + moved).astype(BF16)
-
-    for f in range(OWN):
-        pack(zs, f, jnp.concatenate([after[64 * j + 16 * f:64 * j + 16 * f + 16] for j in range(RB // 16)], axis=0))
-    z_copies = [remote(zs.at[lax.rem(z + d + NZ, OWN)], zr.at[slot], z_send.at[slot], z_recv.at[slot], dz(d))
-                for slot, d in ((3, two), (1, 1), (2, -1))]
-    for copy in z_copies:
-        copy.start()
+    for q, (src, dst, at) in enumerate(spots):
+        x_ref[q] = gather(src, at)
+    fetch[2].wait()
+    own = norm(x_ref[...].reshape(OWN * RB, E)).astype(BF16)
+    fq = nn(own, fw_ref[0]).astype(BF16)
+    fk = nn(own, fw_ref[1]).astype(BF16)
+    fv = nn(own, fw_ref[2]).astype(BF16)
+    z_copies = []
+    for q, (src, dst, at) in enumerate(spots):
+        ex[q].wait_recv()
+        other = norm(gather(dst, at)).astype(BF16)
+        ok = nn(other, fw_ref[1]).astype(BF16)
+        ov = nn(other, fw_ref[2]).astype(BF16)
+        mixes = []
+        for j in range(PR // 16):
+            here, there = slice(64 * j, 64 * j + 64), slice(128 * q + 64 * j, 128 * q + 64 * j + 64)
+            qj = fq[there]
+            kj = jnp.concatenate([fk[there], ok[here]], axis=0)
+            vj = jnp.concatenate([fv[there], ov[here]], axis=0)
+            s = nt(jnp.concatenate([jnp.where(m, qj, zero) for m in masks], axis=0), kj) * SCALE
+            s = jnp.where(same, s, FAR)
+            w = jnp.exp2(s - jnp.max(s, axis=1, keepdims=True))
+            o = nn(w.astype(BF16), vj) / jnp.sum(w, axis=1, keepdims=True)
+            mixed = o[0:64]
+            for head in range(1, HEADS):
+                mixed = jnp.where(masks[head], o[64 * head:64 * head + 64], mixed)
+            mixes.append(mixed.astype(BF16))
+        moved = nn(jnp.concatenate(mixes, axis=0), fw_ref[3]).astype(BF16).astype(F32)
+        after = (x_ref[q] + moved).astype(BF16)
+        for f in range(OWN):
+            part = jnp.concatenate([after[64 * j + 16 * f:64 * j + 16 * f + 16] for j in range(PR // 16)], axis=0)
+            pack_piece(zs, f, q, part)
+        rows = pl.ds(q * PB, PB)
+        for slot, d in ((3, two), (1, 1), (2, -1)):
+            copy = remote(zs.at[lax.rem(z + d + NZ, OWN), rows], zr.at[slot, rows],
+                          z_send.at[slot, q], z_recv.at[slot, q], dz(d))
+            copy.start()
+            z_copies.append(copy)
     zr[0] = zs[lax.rem(z, OWN)]
     for copy in z_copies:
         copy.wait_recv()
@@ -197,9 +203,9 @@
         t, p, a = ORDER[i]
         out = []
         if (p, a) == (0, 0):
-            out += [(2, y_pair, SLOT[t, 1, 0], None, ag_recv)]
-        if a == 0:
-            out += [(0, x_up, SLOT[t, p, 1], None, ag_recv), (1, x_down, SLOT[t, p, 2], None, ag_recv)]
+            out += [(0, x_up, SLOT[t, 0, 1], None, ag_recv), (1, x_down, SLOT[t, 0, 2], None, ag_recv),
+                    (2, y_pair, SLOT[t, 1, 0], None, ag_recv),
+                    (3, d_up, SLOT[t, 1, 1], None, ag_recv), (4, d_down, SLOT[t, 1, 2], None, ag_recv)]
         if a == 1:
             out += [(0, x_up, SLOT[t, p, 3], low, ag_recv)]
         if a == 2:
@@ -261,7 +267,7 @@
     def score(i, u):
         for k in range(2):
             s = nn(half_keys(i, k), qp[u, k])
-            sbuf[u % 3, KB * k:KB * k + KB, :] = s
+            sbuf[u, KB * k:KB * k + KB, :] = s
             m_new[u] = jnp.maximum(m_new[u], jnp.max(s, axis=0, keepdims=True))
 
     def weigh(u):
@@ -269,7 +275,7 @@
         new = m_new[u]
         fade = jnp.exp2(m_acc[u] - new)
         m_acc[u] = new
-        w = jnp.exp2(sbuf[u % 3] - new).astype(BF16)
+        w = jnp.exp2(sbuf[u] - new).astype(BF16)
         acc[u, lo:hi, :] = acc[u, lo:hi, :] * fade + nn(va[u // 3, lo:hi, :], w)
 
     def values(i):
@@ -285,21 +291,23 @@
     def advance(i, following):
         values(i)
         for u in range(UNITS):
-            if u + 2 < UNITS:
-                score(i, u + 2)
+            if u + 3 < UNITS:
+                score(i, u + 3)
             elif following is not None:
-                score(following, u + 2 - UNITS)
+                score(following, u + 3 - UNITS)
             weigh(u)
 
     arrive(0)
     score(0, 0)
     score(0, 1)
+    score(0, 2)
     advance(0, None)
     handle(1)
     handle(2)
     arrive(1)
     score(1, 0)
     score(1, 1)
+    score(1, 2)
 
     def step(i, carry):
         def pick(lo, hi):
@@ -332,19 +340,21 @@
                   jnp.concatenate([o[1][48:80, UW // 2:], o[2][48:80]], axis=1)]
     mix_t = jnp.concatenate(parts, axis=0).astype(BF16)
     mix = nt(eye(NQ), mix_t).astype(BF16)
-    after_row = res[...] + nn(mix, rw_ref[3])
-    n3 = norm(after_row).astype(BF16)
-    hidden = nn(n3, up_ref[...])
-    hidden = (hidden * 0.5 * (1.0 + lax.erf(hidden * (2.0 ** -0.5)))).astype(BF16)
-    out = (after_row + nt(hidden, down_ref[...])).astype(BF16)
-    for k in range(NS):
-        pack(os_ref, k, out[k * RB:(k + 1) * RB])
-
     mine = lax.rem(z, OWN)
-    o_copies = [remote(os_ref.at[slot], or_ref.at[mine], o_send.at[slot], o_recv.at[mine], dz(d))
-                for slot, d in ((3, -two), (1, -1), (2, 1))]
-    for copy in o_copies:
-        copy.start()
+    o_copies = []
+    for slot, d in ((3, -two), (1, -1), (2, 1), (0, 0)):
+        rows = slice(slot * RB, slot * RB + RB)
+        after_row = res[rows, :] + nn(mix[rows], rw_ref[3])
+        n3 = norm(after_row).astype(BF16)
+        hidden = nn(n3, up_ref[...])
+        hidden = (hidden * 0.5 * (1.0 + lax.erf(hidden * (2.0 ** -0.5)))).astype(BF16)
+        out = (after_row + nt(hidden, down_ref[...])).astype(BF16)
+        for q in range(PIECES):
+            pack_piece(os_ref, slot, q, out[q * PR:(q + 1) * PR])
+        if slot:
+            copy = remote(os_ref.at[slot], or_ref.at[mine], o_send.at[slot], o_recv.at[mine], dz(d))
+            copy.start()
+            o_copies.append(copy)
     or_ref[mine] = os_ref[0]
     for d in (1, -1, 2):
         f = lax.rem(z + d + NZ, OWN)
@@ -374,8 +384,7 @@
         scratch_shapes=[pltpu.VMEM(v.shape, BF16) for v in args] + [
             pltpu.VMEM((TR, OWN * E), BF16),
             pltpu.VMEM((TE, OWN * E), BF16),
-            pltpu.VMEM((OWN * RB, E), F32),
-            pltpu.VMEM((OWN * RB, E), F32),
+            pltpu.VMEM((PIECES, OWN * PR, E), F32),
             pltpu.VMEM((OWN, ZB, 128), BF16),
             pltpu.VMEM((NS, ZB, 128), BF16),
             pltpu.VMEM((2 * STEPS, BLOCK, 128), BF16),
@@ -383,15 +392,15 @@
             pltpu.VMEM((UNITS, 2, 256, UW), BF16),
             pltpu.VMEM((2, E, 256), BF16),
             pltpu.VMEM((3, 80, 2 * KB), BF16),
-            pltpu.VMEM((3, 2 * KB, UW), F32),
+            pltpu.VMEM((UNITS, 2 * KB, UW), F32),
             pltpu.VMEM((UNITS, 80, UW), F32),
             pltpu.VMEM((UNITS, 1, UW), F32),
             pltpu.VMEM((UNITS, 1, UW), F32),
             pltpu.VMEM((NS, ZB, 128), BF16),
             pltpu.VMEM((OWN, ZB, 128), BF16),
             pltpu.VMEM((NQ, E), F32),
-            dma((2,)), dma((2,)), dma((NS,)), dma((NS,)),
-            dma((STEPS, 4)), dma((STEPS,)), dma((STEPS,)), dma((STEPS,)), dma((STEPS,)),
+            dma((PIECES,)), dma((PIECES,)), dma((NS, PIECES)), dma((NS, PIECES)),
+            dma((STEPS, 5)), dma((STEPS,)), dma((STEPS,)), dma((STEPS,)), dma((STEPS,)),
             dma((NS,)), dma((OWN,)), dma((2,)), dma((1,)), dma((6,)),
         ],
         compiler_params=pltpu.CompilerParams(

time: 59.3 us -> 62.5 us (1.054)
  Pallas kernels: 57.3 us -> 60.5 us
    pallas_call x1, Pallas kernels: 57.3 us -> 60.5 us  [body(): pl.pallas_call(kernel, name='layer', out_shape=(pltpu.VMEM(train.shape, B...]
where the time goes in v6:
time: 62.5 us; the launch traced here: 62.4 us
  Pallas kernels  60.5 us (97%)
  local copies, waits for them, and re-layouts  1.26 us (2%)
  between operations  0.64 us (1%)
    pallas_call x1, Pallas kernels, body(): pl.pallas_call(kernel, name='layer', out_shape=(pltpu.VMEM(train.shape, B...  60.5 us
    unnamed x2, local copies, waits for them, and re-layouts  1.26 us

profile of v6, /device:TPU:1, one launch (start us, length us, event | category | flops | bytes accessed | tf_op | source)
XLA Modules:
  0.0 62.4 jit_solution(5289495873586907144)
XLA Ops:
  0.6 60.5 %layer.1 = (bf16[64,768]{1,0:T(8,128)(2,1)S(1)}, bf16[32,768]{1,0:T(8,128)(2,1)S(1)}) custom-call(bf16[64,768]{1,0:T(8,128)(2,1)} %train_in.1, bf16[32,768]{1,0:T(8,128)(2,1)} %test_in.1, bf16[4,192,192]{2,1,0:T(8,128)(2,1)} %fw_in.1, bf16[4,192,192]{2,1,0:T(8,128)(2,1)} %rw_in.1, bf16[192,768]{1,0:T(8,128)(2,1)} %up_in.1, bf16[192,768]{1,0:T(8,128)(2,1)} %bitcast.1), custom_call_target="tpu_custom_call" | custom-call | tf_op jit(solution)/shard_map/layer/pallas_call | solution.py:378
  61.1 0.6 %copy.10 = bf16[64,768]{1,0:T(8,128)(2,1)} copy(bf16[64,768]{1,0:T(8,128)(2,1)S(1)} %get-tuple-element.2) | data formatting | bytes 196608
  61.7 0.6 copy.11

commit v7 on v5

--- a/solution.py
+++ b/solution.py
@@ -30,11 +30,10 @@
 BLOCK = KB * 3 // 2
 HALF = BLOCK // 2
 
-ORDER = [(0, 0, 0), (0, 1, 0), (0, 0, 1), (0, 0, 2), (0, 1, 1), (0, 1, 2), (0, 0, 3), (0, 1, 3),
-         (1, 0, 0), (1, 1, 0), (1, 0, 1), (1, 0, 2), (1, 1, 1), (1, 1, 2), (1, 0, 3), (1, 1, 3)]
+ORDER = [(0, 0, 0), (0, 1, 0), (0, 0, 1), (0, 0, 2), (0, 1, 1), (0, 1, 2), (1, 0, 0), (0, 0, 3),
+         (0, 1, 3), (1, 1, 0), (1, 0, 1), (1, 0, 2), (1, 1, 1), (1, 1, 2), (1, 0, 3), (1, 1, 3)]
 SLOT = {pos: i for i, pos in enumerate(ORDER)}
 STEPS = len(ORDER)
-RELAY = 4
 UW = 256
 UNITS = HEADS * NQ // UW
 
@@ -82,9 +81,9 @@
 def kernel(train_in, test_in, fw_in, rw_in, up_in, down_in,
            train_out, test_out,
            train_ref, test_ref, fw_ref, rw_ref, up_ref, down_ref,
-           cell_tr, cell_te, x_ref, x2_ref, zs, zr, kbuf, relay, qp, wv, va, sbuf, acc, m_acc, m_new, os_ref, or_ref, res,
+           cell_tr, cell_te, x_ref, x2_ref, zs, zr, kbuf, qp, wv, va, sbuf, acc, m_acc, m_new, os_ref, or_ref, res,
            ex_send, ex_recv, z_send, z_recv, own_send, sib_send, ag_recv, ag_recv2, sib_recv,
-           o_send, o_recv, rel_send, rel_recv, in_sem):
+           o_send, o_recv, far_send, in_sem):
     r = lax.axis_index("rows")
     h = lax.axis_index("feat")
     c = lax.rem(r, NC)
@@ -105,7 +104,6 @@
     sibling = dev(x, y, z, 1 - c)
     partner = dev(x, lax.rem(y + 2, NY), z, c)
     two = jnp.where(lax.rem(z, 2) == 0, 2, -2)
-    hop = jnp.where(c == 0, 2, -2)
 
     barrier = pltpu.get_barrier_semaphore()
     peers = (partner, dz(2), dz(-2), dz(1), dz(-1), x_up, x_down, y_pair, sibling)
@@ -209,8 +207,7 @@
     def sib_copy(i):
         return remote(kbuf.at[i], kbuf.at[STEPS + i], sib_send.at[i], sib_recv.at[i], sibling)
 
-    via = remote(kbuf.at[0], relay, rel_send.at[0], rel_recv.at[0], dz(hop))
-    onward = remote(relay, kbuf.at[SLOT[1, 0, 0]], rel_send.at[1], ag_recv.at[SLOT[1, 0, 0]], dz(hop))
+    across = remote(kbuf.at[0], kbuf.at[SLOT[1, 0, 0]], far_send.at[0], ag_recv.at[SLOT[1, 0, 0]], dz(4))
 
     def handle(i):
         t, p, a = ORDER[i]
@@ -224,7 +221,7 @@
             copy.start()
         sib_copy(i).start()
 
-    via.start()
+    across.start()
     handle(0)
 
     fetch[3].wait()
@@ -253,15 +250,22 @@
 
     span = [(0, 48), (0, 80), (32, 80)]
 
+    def blocks_of(i):
+        if isinstance(i, int) and i == 0:
+            return 0, STEPS
+        one = jnp.where(i < STEPS - 1, i + 1, 2 * STEPS - 1)
+        other = jnp.where(i == 1, 1, i + STEPS - 1)
+        return (jnp.where(i == 3, STEPS + 3, jnp.where(i == 4, 4, one)), jnp.where(i == 4, 5, other))
+
     def half_keys(i, k):
         return jnp.concatenate([
-            jnp.concatenate([kbuf[i + STEPS * p, 128 * k:128 * k + 128, :], kbuf[i + STEPS * p, KB:BLOCK, :]], axis=1)
-            for p in range(2)], axis=0)
+            jnp.concatenate([kbuf[slot, 128 * k:128 * k + 128, :], kbuf[slot, KB:BLOCK, :]], axis=1)
+            for slot in blocks_of(i)], axis=0)
 
     def score(i, u):
         for k in range(2):
             s = nn(half_keys(i, k), qp[u, k])
-            sbuf[u % 3, KB * k:KB * k + KB, :] = s
+            sbuf[u, KB * k:KB * k + KB, :] = s
             m_new[u] = jnp.maximum(m_new[u], jnp.max(s, axis=0, keepdims=True))
 
     def weigh(u):
@@ -269,7 +273,7 @@
         new = m_new[u]
         fade = jnp.exp2(m_acc[u] - new)
         m_acc[u] = new
-        w = jnp.exp2(sbuf[u % 3] - new).astype(BF16)
+        w = jnp.exp2(sbuf[u] - new).astype(BF16)
         acc[u, lo:hi, :] = acc[u, lo:hi, :] * fade + nn(va[u // 3, lo:hi, :], w)
 
     def values(i):
@@ -284,30 +288,37 @@
 
     def advance(i, following):
         values(i)
+        order = []
         for u in range(UNITS):
-            if u + 2 < UNITS:
-                score(i, u + 2)
+            order += [("s", u + 3), ("w", u)]
+        seq = []
+        for u in range(0, UNITS, 2):
+            chunk = [u] + ([u + 1] if u + 1 < UNITS else [])
+            seq += [("s", v + 3) for v in chunk] + [("w", v) for v in chunk]
+        for kind, u in seq:
+            if kind == "w":
+                weigh(u)
+            elif u < UNITS:
+                score(i, u)
             elif following is not None:
-                score(following, u + 2 - UNITS)
-            weigh(u)
+                score(following, u - UNITS)
 
     arrive(0)
     score(0, 0)
     score(0, 1)
+    score(0, 2)
     advance(0, None)
     handle(1)
     handle(2)
-    arrive(1)
     score(1, 0)
     score(1, 1)
+    score(1, 2)
 
     def step(i, carry):
         def pick(lo, hi):
             if hi - lo == 1:
-                if lo + 2 == RELAY:
-                    via.wait_recv()
-                    onward.start()
-                handle(lo + 2)
+                for k in {2: (), 3: (4, 5)}.get(lo, (lo + 2,)):
+                    handle(k)
                 return
             mid = (lo + hi) // 2
             pl.when(i < mid)(lambda: pick(lo, mid))
@@ -315,7 +326,11 @@
 
         pl.when(i < STEPS - 2)(lambda: pick(1, STEPS - 2))
 
-        @pl.when(i < STEPS - 1)
+        @pl.when((i != 3) & (i < STEPS - 1))
+        def _():
+            arrive(i)
+
+        @pl.when((i == 2) | (i == STEPS - 2))
         def _():
             arrive(i + 1)
 
@@ -353,7 +368,7 @@
     train_out[...] = jnp.concatenate([v[0:TR] for v in blocks], axis=1)
     test_out[...] = jnp.concatenate([v[TR:RB] for v in blocks], axis=1)
 
-    for copy in ex + z_copies + o_copies + [via, onward]:
+    for copy in ex + z_copies + o_copies + [across]:
         copy.wait_send()
     for i in range(STEPS):
         for copy in sends(i):
@@ -379,11 +394,10 @@
             pltpu.VMEM((OWN, ZB, 128), BF16),
             pltpu.VMEM((NS, ZB, 128), BF16),
             pltpu.VMEM((2 * STEPS, BLOCK, 128), BF16),
-            pltpu.VMEM((BLOCK, 128), BF16),
             pltpu.VMEM((UNITS, 2, 256, UW), BF16),
             pltpu.VMEM((2, E, 256), BF16),
             pltpu.VMEM((3, 80, 2 * KB), BF16),
-            pltpu.VMEM((3, 2 * KB, UW), F32),
+            pltpu.VMEM((UNITS, 2 * KB, UW), F32),
             pltpu.VMEM((UNITS, 80, UW), F32),
             pltpu.VMEM((UNITS, 1, UW), F32),
             pltpu.VMEM((UNITS, 1, UW), F32),
@@ -392,7 +406,7 @@
             pltpu.VMEM((NQ, E), F32),
             dma((2,)), dma((2,)), dma((NS,)), dma((NS,)),
             dma((STEPS, 4)), dma((STEPS,)), dma((STEPS,)), dma((STEPS,)), dma((STEPS,)),
-            dma((NS,)), dma((OWN,)), dma((2,)), dma((1,)), dma((6,)),
+            dma((NS,)), dma((OWN,)), dma((1,)), dma((6,)),
         ],
         compiler_params=pltpu.CompilerParams(
             collective_id=0, has_side_effects=True, vmem_limit_bytes=60 * 1024 * 1024),

time: 59.3 us -> 55.9 us (0.943)
  Pallas kernels: 57.3 us -> 53.9 us
    pallas_call x1, Pallas kernels: 57.3 us -> 53.9 us  [body(): pl.pallas_call(kernel, name='layer', out_shape=(pltpu.VMEM(train.shape, B...]
where the time goes in v7:
time: 55.9 us; the launch traced here: 55.8 us
  Pallas kernels  53.9 us (96%)
  local copies, waits for them, and re-layouts  1.26 us (2%)
  between operations  0.64 us (1%)
    pallas_call x1, Pallas kernels, body(): pl.pallas_call(kernel, name='layer', out_shape=(pltpu.VMEM(train.shape, B...  53.9 us
    unnamed x2, local copies, waits for them, and re-layouts  1.26 us

profile of v7, /device:TPU:1, one launch (start us, length us, event | category | flops | bytes accessed | tf_op | source)
XLA Modules:
  0.0 55.8 jit_solution(18358529657539115295)
XLA Ops:
  0.6 53.9 %layer.1 = (bf16[64,768]{1,0:T(8,128)(2,1)S(1)}, bf16[32,768]{1,0:T(8,128)(2,1)S(1)}) custom-call(bf16[64,768]{1,0:T(8,128)(2,1)} %train_in.1, bf16[32,768]{1,0:T(8,128)(2,1)} %test_in.1, bf16[4,192,192]{2,1,0:T(8,128)(2,1)} %fw_in.1, bf16[4,192,192]{2,1,0:T(8,128)(2,1)} %rw_in.1, bf16[192,768]{1,0:T(8,128)(2,1)} %up_in.1, bf16[192,768]{1,0:T(8,128)(2,1)} %bitcast.1), custom_call_target="tpu_custom_call" | custom-call | tf_op jit(solution)/shard_map/layer/pallas_call | solution.py:383
  54.5 0.6 %copy.10 = bf16[64,768]{1,0:T(8,128)(2,1)} copy(bf16[64,768]{1,0:T(8,128)(2,1)S(1)} %get-tuple-element.2) | data formatting | bytes 196608
  55.1 0.6 %copy.11 = bf16[32,768]{1,0:T(8,128)(2,1)} copy(bf16[32,768]{1,0:T(8,128)(2,1)S(1)} %get-tuple-element.3) | data formatting | bytes 98304

commit v8 on v7

--- a/solution.py
+++ b/solution.py
@@ -288,20 +288,12 @@
 
     def advance(i, following):
         values(i)
-        order = []
         for u in range(UNITS):
-            order += [("s", u + 3), ("w", u)]
-        seq = []
-        for u in range(0, UNITS, 2):
-            chunk = [u] + ([u + 1] if u + 1 < UNITS else [])
-            seq += [("s", v + 3) for v in chunk] + [("w", v) for v in chunk]
-        for kind, u in seq:
-            if kind == "w":
-                weigh(u)
-            elif u < UNITS:
-                score(i, u)
+            if u + 3 < UNITS:
+                score(i, u + 3)
             elif following is not None:
-                score(following, u - UNITS)
+                score(following, u + 3 - UNITS)
+            weigh(u)
 
     arrive(0)
     score(0, 0)

time: 55.9 us -> 55.3 us (0.989)
  Pallas kernels: 53.9 us -> 53.3 us
where the time goes in v8:
time: 55.3 us; the launch traced here: 55.2 us
  Pallas kernels  53.3 us (96%)
  local copies, waits for them, and re-layouts  1.26 us (2%)
  between operations  0.64 us (1%)
    pallas_call x1, Pallas kernels, body(): pl.pallas_call(kernel, name='layer', out_shape=(pltpu.VMEM(train.shape, B...  53.3 us
    unnamed x2, local copies, waits for them, and re-layouts  1.26 us

profile of v8, /device:TPU:1, one launch (start us, length us, event | category | flops | bytes accessed | tf_op | source)
XLA Modules:
  0.0 55.2 jit_solution(4643498514289568705)
XLA Ops:
  0.6 53.3 %layer.1 = (bf16[64,768]{1,0:T(8,128)(2,1)S(1)}, bf16[32,768]{1,0:T(8,128)(2,1)S(1)}) custom-call(bf16[64,768]{1,0:T(8,128)(2,1)} %train_in.1, bf16[32,768]{1,0:T(8,128)(2,1)} %test_in.1, bf16[4,192,192]{2,1,0:T(8,128)(2,1)} %fw_in.1, bf16[4,192,192]{2,1,0:T(8,128)(2,1)} %rw_in.1, bf16[192,768]{1,0:T(8,128)(2,1)} %up_in.1, bf16[192,768]{1,0:T(8,128)(2,1)} %bitcast.1), custom_call_target="tpu_custom_call" | custom-call | tf_op jit(solution)/shard_map/layer/pallas_call | solution.py:375
  54.0 0.6 %copy.10 = bf16[64,768]{1,0:T(8,128)(2,1)} copy(bf16[64,768]{1,0:T(8,128)(2,1)S(1)} %get-tuple-element.2) | data formatting | bytes 196608
  54.6 0.6 %copy.11 = bf16[32,768]{1,0:T(8,128)(2,1)} copy(bf16[32,768]{1,0:T(8,128)(2,1)S(1)} %get-tuple-element.3) | data formatting | bytes 98304

commit v9 on v8

--- a/solution.py
+++ b/solution.py
@@ -165,10 +165,15 @@
             mixed = jnp.where(masks[head], o[64 * head:64 * head + 64], mixed)
         mixes.append(mixed.astype(BF16))
     moved = nn(jnp.concatenate(mixes, axis=0), fw_ref[3]).astype(BF16).astype(F32)
-    after = (x_ref[...] + moved).astype(BF16)
+    after = x_ref[...] + moved
+    normed = norm(after).astype(BF16)
+
+    def rows_of(v, f):
+        return jnp.concatenate([v[64 * j + 16 * f:64 * j + 16 * f + 16] for j in range(RB // 16)], axis=0)
 
     for f in range(OWN):
-        pack(zs, f, jnp.concatenate([after[64 * j + 16 * f:64 * j + 16 * f + 16] for j in range(RB // 16)], axis=0))
+        pack(zs, f, rows_of(normed, f))
+        res[f * RB:(f + 1) * RB, :] = rows_of(after, f)
     z_copies = [remote(zs.at[lax.rem(z + d + NZ, OWN)], zr.at[slot], z_send.at[slot], z_recv.at[slot], dz(d))
                 for slot, d in ((3, two), (1, 1), (2, -1))]
     for copy in z_copies:
@@ -177,9 +182,7 @@
     for copy in z_copies:
         copy.wait_recv()
 
-    for k in range(NS):
-        res[k * RB:(k + 1) * RB, :] = unpack(zr, k).astype(F32)
-    n2 = norm(res[...]).astype(BF16)
+    n2 = jnp.concatenate([unpack(zr, k) for k in range(NS)], axis=0)
     keys = jnp.concatenate([n2[k * RB:k * RB + TR] for k in range(NS)], axis=0)
     kbuf[0, 0:KB, :] = keys[:, 0:128]
     kbuf[0, KB:BLOCK, :] = jnp.concatenate([keys[0:KB // 2, 128:E], keys[KB // 2:KB, 128:E]], axis=1)
@@ -339,13 +342,8 @@
                   jnp.concatenate([o[1][48:80, UW // 2:], o[2][48:80]], axis=1)]
     mix_t = jnp.concatenate(parts, axis=0).astype(BF16)
     mix = nt(eye(NQ), mix_t).astype(BF16)
-    after_row = res[...] + nn(mix, rw_ref[3])
-    n3 = norm(after_row).astype(BF16)
-    hidden = nn(n3, up_ref[...])
-    hidden = (hidden * 0.5 * (1.0 + lax.erf(hidden * (2.0 ** -0.5)))).astype(BF16)
-    out = (after_row + nt(hidden, down_ref[...])).astype(BF16)
     for k in range(NS):
-        pack(os_ref, k, out[k * RB:(k + 1) * RB])
+        pack(os_ref, k, mix[k * RB:(k + 1) * RB])
 
     mine = lax.rem(z, OWN)
     o_copies = [remote(os_ref.at[slot], or_ref.at[mine], o_send.at[slot], o_recv.at[mine], dz(d))
@@ -356,7 +354,13 @@
     for d in (1, -1, 2):
         f = lax.rem(z + d + NZ, OWN)
         remote(os_ref.at[0], or_ref.at[f], o_send.at[0], o_recv.at[f], sibling).wait_recv()
-    blocks = [unpack(or_ref, f) for f in range(OWN)]
+    mix = jnp.concatenate([unpack(or_ref, f) for f in range(OWN)], axis=0)
+    after_row = res[...] + nn(mix, rw_ref[3])
+    n3 = norm(after_row).astype(BF16)
+    hidden = nn(n3, up_ref[...])
+    hidden = (hidden * 0.5 * (1.0 + lax.erf(hidden * (2.0 ** -0.5)))).astype(BF16)
+    out = (after_row + nt(hidden, down_ref[...])).astype(BF16)
+    blocks = [out[f * RB:(f + 1) * RB] for f in range(OWN)]
     train_out[...] = jnp.concatenate([v[0:TR] for v in blocks], axis=1)
     test_out[...] = jnp.concatenate([v[TR:RB] for v in blocks], axis=1)
 

time: 55.3 us -> 55.4 us (level)
  no operation moved by 1% of the time
where the time goes in v9:
time: 55.4 us; the launch traced here: 55.3 us
  Pallas kernels  53.4 us (96%)
  local copies, waits for them, and re-layouts  1.26 us (2%)
  between operations  0.64 us (1%)
    pallas_call x1, Pallas kernels, body(): pl.pallas_call(kernel, name='layer', out_shape=(pltpu.VMEM(train.shape, B...  53.4 us
    unnamed x2, local copies, waits for them, and re-layouts  1.26 us

profile of v9, /device:TPU:1, one launch (start us, length us, event | category | flops | bytes accessed | tf_op | source)
XLA Modules:
  0.0 55.3 jit_solution(11654555685525333589)
XLA Ops:
  0.6 53.4 %layer.1 = (bf16[64,768]{1,0:T(8,128)(2,1)S(1)}, bf16[32,768]{1,0:T(8,128)(2,1)S(1)}) custom-call(bf16[64,768]{1,0:T(8,128)(2,1)} %train_in.1, bf16[32,768]{1,0:T(8,128)(2,1)} %test_in.1, bf16[4,192,192]{2,1,0:T(8,128)(2,1)} %fw_in.1, bf16[4,192,192]{2,1,0:T(8,128)(2,1)} %rw_in.1, bf16[192,768]{1,0:T(8,128)(2,1)} %up_in.1, bf16[192,768]{1,0:T(8,128)(2,1)} %bitcast.1), custom_call_target="tpu_custom_call" | custom-call | tf_op jit(solution)/shard_map/layer/pallas_call | solution.py:379
  54.0 0.6 %copy.10 = bf16[64,768]{1,0:T(8,128)(2,1)} copy(bf16[64,768]{1,0:T(8,128)(2,1)S(1)} %get-tuple-element.2) | data formatting | bytes 196608
  54.6 0.6 %copy.11 = bf16[32,768]{1,0:T(8,128)(2,1)} copy(bf16[32,768]{1,0:T(8,128)(2,1)S(1)} %get-tuple-element.3) | data formatting | bytes 98304

commit v10 on v9

--- a/solution.py
+++ b/solution.py
@@ -81,7 +81,7 @@
 def kernel(train_in, test_in, fw_in, rw_in, up_in, down_in,
            train_out, test_out,
            train_ref, test_ref, fw_ref, rw_ref, up_ref, down_ref,
-           cell_tr, cell_te, x_ref, x2_ref, zs, zr, kbuf, qp, wv, va, sbuf, acc, m_acc, m_new, os_ref, or_ref, res,
+           cell_tr, cell_te, x_ref, x2_ref, zs, zr, kbuf, qp, wv, va, sbuf, acc, m_acc, m_new, os_ref, or_ref, res, fin,
            ex_send, ex_recv, z_send, z_recv, own_send, sib_send, ag_recv, ag_recv2, sib_recv,
            o_send, o_recv, far_send, in_sem):
     r = lax.axis_index("rows")
@@ -350,19 +350,21 @@
                 for slot, d in ((3, -two), (1, -1), (2, 1))]
     for copy in o_copies:
         copy.start()
-    or_ref[mine] = os_ref[0]
+
+    def finish(f, mixture):
+        after_row = res[pl.ds(pl.multiple_of(f * RB, RB), RB), :] + nn(mixture, rw_ref[3])
+        n3 = norm(after_row).astype(BF16)
+        hidden = nn(n3, up_ref[...])
+        hidden = (hidden * 0.5 * (1.0 + lax.erf(hidden * (2.0 ** -0.5)))).astype(BF16)
+        fin[f] = (after_row + nt(hidden, down_ref[...])).astype(BF16)
+
+    finish(mine, mix[0:RB])
     for d in (1, -1, 2):
         f = lax.rem(z + d + NZ, OWN)
         remote(os_ref.at[0], or_ref.at[f], o_send.at[0], o_recv.at[f], sibling).wait_recv()
-    mix = jnp.concatenate([unpack(or_ref, f) for f in range(OWN)], axis=0)
-    after_row = res[...] + nn(mix, rw_ref[3])
-    n3 = norm(after_row).astype(BF16)
-    hidden = nn(n3, up_ref[...])
-    hidden = (hidden * 0.5 * (1.0 + lax.erf(hidden * (2.0 ** -0.5)))).astype(BF16)
-    out = (after_row + nt(hidden, down_ref[...])).astype(BF16)
-    blocks = [out[f * RB:(f + 1) * RB] for f in range(OWN)]
-    train_out[...] = jnp.concatenate([v[0:TR] for v in blocks], axis=1)
-    test_out[...] = jnp.concatenate([v[TR:RB] for v in blocks], axis=1)
+        finish(f, unpack(or_ref, f))
+    train_out[...] = jnp.concatenate([fin[f, 0:TR, :] for f in range(OWN)], axis=1)
+    test_out[...] = jnp.concatenate([fin[f, TR:RB, :] for f in range(OWN)], axis=1)
 
     for copy in ex + z_copies + o_copies + [across]:
         copy.wait_send()
@@ -400,6 +402,7 @@
             pltpu.VMEM((NS, ZB, 128), BF16),
             pltpu.VMEM((OWN, ZB, 128), BF16),
             pltpu.VMEM((NQ, E), F32),
+            pltpu.VMEM((OWN, RB, E), BF16),
             dma((2,)), dma((2,)), dma((NS,)), dma((NS,)),
             dma((STEPS, 4)), dma((STEPS,)), dma((STEPS,)), dma((STEPS,)), dma((STEPS,)),
             dma((NS,)), dma((OWN,)), dma((1,)), dma((6,)),

time: 55.4 us -> 55.8 us (level)
  no operation moved by 1% of the time
where the time goes in v10:
time: 55.8 us; the launch traced here: 55.7 us
  Pallas kernels  53.8 us (96%)
  local copies, waits for them, and re-layouts  1.26 us (2%)
  between operations  0.64 us (1%)
    pallas_call x1, Pallas kernels, body(): pl.pallas_call(kernel, name='layer', out_shape=(pltpu.VMEM(train.shape, B...  53.8 us
    unnamed x2, local copies, waits for them, and re-layouts  1.26 us

profile of v10, /device:TPU:1, one launch (start us, length us, event | category | flops | bytes accessed | tf_op | source)
XLA Modules:
  0.0 55.7 jit_solution(14393977196913565548)
XLA Ops:
  0.6 53.8 %layer.1 = (bf16[64,768]{1,0:T(8,128)(2,1)S(1)}, bf16[32,768]{1,0:T(8,128)(2,1)S(1)}) custom-call(bf16[64,768]{1,0:T(8,128)(2,1)} %train_in.1, bf16[32,768]{1,0:T(8,128)(2,1)} %test_in.1, bf16[4,192,192]{2,1,0:T(8,128)(2,1)} %fw_in.1, bf16[4,192,192]{2,1,0:T(8,128)(2,1)} %rw_in.1, bf16[192,768]{1,0:T(8,128)(2,1)} %up_in.1, bf16[192,768]{1,0:T(8,128)(2,1)} %bitcast.1), custom_call_target="tpu_custom_call" | custom-call | tf_op jit(solution)/shard_map/layer/pallas_call | solution.py:381
  54.4 0.6 %copy.10 = bf16[64,768]{1,0:T(8,128)(2,1)} copy(bf16[64,768]{1,0:T(8,128)(2,1)S(1)} %get-tuple-element.2) | data formatting | bytes 196608
  55.0 0.6 %copy.11 = bf16[32,768]{1,0:T(8,128)(2,1)} copy(bf16[32,768]{1,0:T(8,128)(2,1)S(1)} %get-tuple-element.3) | data formatting | bytes 98304
